TPU v7x, 128 devices: a whole 4x4x4 slice. The times are simulated.
128 devices in a mesh: row: 32 (over y, x, core), col: 4 (over z).
Axes of the slice: x: 4, y: 4, z: 4, core: 2. Of those that a mesh axis runs over, the one named last changes fastest.
Arguments:
- coeffs: bfloat16 [6144, 4096], P('row', 'col'), may hold values from -0.00390625 to 0.00390625
- occupation: float32 [4096], P('col'), may hold values from 0.5 to 2
- basis_on_grid: bfloat16 [1280, 512, 512], P('row'), may hold values from -6 to 6
- basis_map: int32 [1280, 512], P('row'), may hold values from 0 to 6143, as said below
- basis_count: int32 [1280], P('row'), may hold values from 256 to 512
- batch_atom: int32 [1280], P('row'), may hold values from 0 to 63
- harmonics: float32 [1280, 49, 512], P('row'), may hold values from -0.25 to 0.25
Outputs:
- density: float32 [1280, 512], P('row', 'col')
- moments: float32 [64, 49], replicated
Inputs may be any that keep to these rules, and one draw needn't show every extreme that they name: `basis_map`: the slots of one batch name distinct basis functions. With R = 192 and o = b // 40, batch b names only basis functions q * R + (o * 96 + w) mod R with 0 <= q < 32 and 0 <= w < 96.
All inputs are finite; a program needn't handle non-finite values.
Results may differ from a plain program's by a relative error of at most 0.0003.
Values may be sent and summed in bfloat16 or wider, within the bound.
A program may use at most 192 MiB of HBM per device.

v0:
```python
import jax
import jax.numpy as jnp
from jax import lax
from jax.sharding import PartitionSpec as P

NATOM = 64


def sent_to_all(shard, axis):
    copies = jnp.broadcast_to(shard, (lax.axis_size(axis), *shard.shape))
    return lax.all_to_all(copies, axis, split_axis=0, concat_axis=0, tiled=True)


def over_copies(shard, axis):
    everything = sent_to_all(shard, axis)
    return jnp.sum(everything, axis=0)


def shards(coeffs, occupation, basis_on_grid, basis_map, basis_count, batch_atom, harmonics):
    batches, points, slots = basis_on_grid.shape
    whole = lax.all_gather(coeffs, "row", axis=0, tiled=True)
    selected = jnp.take(whole, basis_map, axis=0)
    slot_ids = lax.broadcasted_iota(jnp.int32, (batches, slots), 1)
    keep = slot_ids < basis_count[:, None]
    masked = jnp.where(keep[:, None, :], basis_on_grid, jnp.zeros_like(basis_on_grid))
    orbital = jnp.einsum("bps,bsk->bpk", masked, selected, preferred_element_type=jnp.float32)
    partial_density = jnp.sum(orbital * orbital * occupation[None, None, :], axis=2)
    atom_ids = lax.broadcasted_iota(jnp.int32, (batches, NATOM), 1)
    member = (batch_atom[:, None] == atom_ids).astype(jnp.float32)
    full_density = over_copies(partial_density, "col")
    local_moment = jnp.einsum(
        "blp,bp->bl", harmonics, full_density, precision=lax.Precision.HIGHEST
    )
    atom_part = jnp.dot(member.T, local_moment, precision=lax.Precision.HIGHEST)
    moments = over_copies(atom_part, "row")
    share = points // lax.axis_size("col")
    density = lax.dynamic_slice_in_dim(full_density, lax.axis_index("col") * share, share, 1)
    return (density, moments)


def solution(mesh):
    placed = (
        P("row", "col"),
        P("col"),
        P("row", None, None),
        P("row", None),
        P("row"),
        P("row"),
        P("row", None, None),
    )
    return jax.shard_map(
        shards, mesh=mesh, in_specs=placed, out_specs=(P("row", "col"), P()), check_vma=False
    )
```

profile of v0, /device:TPU:0, one launch (start us, length us, event | category | flops | bytes accessed | tf_op | source)
XLA Modules:
  0.0 257.3 jit_solution(1520194988948494849)
XLA Ops:
  7.2 0.0 all-gather.2.cloned.1.call-start
  7.2 0.7 all-gather.2.cloned.1.call-update
  7.9 0.9 fusion.14
  8.8 1.0 iota_compare_fusion
  9.8 0.0 copy-start
  9.9 65.6 %all-gather.2.cloned.1.call-done = bf16[6144,1024]{1,0:T(8,128)(2,1)} async-done(((bf16[192,1024]{1,0:T(8,128)(2,1)}), bf16[6144,1024]{1,0:T(8,128)(2,1)}) %all-gather.2.cloned.1.call-update) | async-done | bytes 12582928 | tf_op jit(solution)/shard_map/all_gather | solution.py:21
  75.4 106.1 %gather_fusion = bf16[20480,1024]{1,0:T(8,128)(2,1)} fusion(bf16[6144,1024]{1,0:T(8,128)(2,1)} %all-gather.2.cloned.1.call-done, s32[20480]{0:T(1024)S(1)} %broadcast_clamp_fusion), kind=kCustom, calls=%fused_computation | custom fusion | bytes 83968000 | tf_op jit(solution)/shard_map/jit(_take)/gather | solution.py:22
  181.6 0.0 copy-done
  181.6 0.0 copy-start.1
  181.6 28.6 %multiply_reduce_fusion = f32[40,512]{1,0:T(8,128)S(1)} fusion(f32[1024]{0:T(1024)S(1)} %copy-done, bf16[40,512,1024]{2,1,0:T(8,128)(2,1)} %bitcast.12, pred[40,512]{1,0:T(8,128)(4,1)S(1)} %get-tuple-element.3, bf16[40,512,512]{2,1,0:T(8,128)(2,1)} %param.9, pred[40,512]{1,0:T(8,128)(4,1)S(1)} %get-tuple-element.2), kind=kOutput, calls=%fused_computation.1 | convolution fusion | flops 21569187840 | bytes 63041536 | tf_op jit(solution)/shard_map/bps,bsk->bpk/dot_general | solution.py:26
  210.2 12.0 %all_to_all.10 = f32[4,40,512]{2,1,0:T(8,128)S(1)} all-to-all(f32[4,40,512]{2,1,0:T(8,128)S(1)} %broadcast_in_dim.38), channel_id=1, replica_groups=mesh['row'=32,'col'=4] {'col'}, dimensions={0} | all-to-all | bytes 655360 | tf_op jit(solution)/shard_map/all_to_all | solution.py:11
  222.2 7.8 %fusion.11 = f32[40,1,49]{2,1,0:T(1,128)S(1)} fusion(f32[40,49,512]{2,0,1:T(8,128)} %param.13, f32[40,512,1]{1,0,2:T(8,128)S(1)} %bitcast.13), kind=kOutput, calls=%fused_computation.9 | convolution fusion | flops 12042240 | bytes 4103840 | tf_op jit(solution)/shard_map/blp,bp->bl/dot_general | solution.py:31
  230.1 0.0 copy-done.1
  230.1 0.2 fusion.15
  230.3 0.1 broadcast_bitcast_fusion
  230.4 1.3 reshape.38
  231.7 5.4 %all-to-all-start.1 = ((f32[32,1,3136]{2,1,0:T(1,128)}), f32[32,1,3136]{2,1,0:T(1,128)S(1)}, u32[]{:S(2)}, u32[]{:S(2)}) async-start(f32[32,1,3136]{2,1,0:T(1,128)} %reshape.38), calls=%async_computation.1 | async-start | bytes 819200 | tf_op jit(solution)/shard_map/all_to_all | solution.py:11
  237.1 0.6 constant_dynamic-slice_fusion
  237.7 9.7 %all-to-all-done.1 = f32[32,1,3136]{2,1,0:T(1,128)S(1)} async-done(((f32[32,1,3136]{2,1,0:T(1,128)}), f32[32,1,3136]{2,1,0:T(1,128)S(1)}, u32[]{:S(2)}, u32[]{:S(2)}) %all-to-all-start.1) | async-done | bytes 401440 | tf_op jit(solution)/shard_map/all_to_all | solution.py:11
  247.5 0.5 broadcast.16
  248.0 1.6 reduce
  249.6 0.2 reshape.39
  249.8 0.7 bitcast_reduce_fusion
  (4 shorter events, 0.1 us)
Async XLA Ops:
  7.2 68.3 %all-gather.2.cloned.1.call-start = ((), (), s32[]{:S(2)}) async-start(), calls=%async_computation.2 | async-start | bytes 12976128 | tf_op jit(solution)/shard_map/all_gather | solution.py:21
  9.8 171.7 %copy-start = (f32[1024]{0:T(1024)S(1)}, f32[1024]{0:T(1024)}, u32[]{:S(2)}) copy-start(f32[1024]{0:T(1024)} %param.8) | copy-start | bytes 12292
  181.6 48.5 %copy-start.1 = (s32[40]{0:T(128)S(1)}, s32[40]{0:T(128)}, u32[]{:S(2)}) copy-start(s32[40]{0:T(128)} %param.12) | copy-start | bytes 484
  231.7 15.8 %all-to-all-start.1 = ((f32[32,1,3136]{2,1,0:T(1,128)}), f32[32,1,3136]{2,1,0:T(1,128)S(1)}, u32[]{:S(2)}, u32[]{:S(2)}) async-start(f32[32,1,3136]{2,1,0:T(1,128)} %reshape.38), calls=%async_computation.1 | async-start | bytes 819200 | tf_op jit(solution)/shard_map/all_to_all | solution.py:11
Sparse Core Ops, SparseCore 0:
  10.2 65.1 all-gather.1
where the time goes:
time: 259 us; the launch traced here: 257 us
  local copies, waits for them, and re-layouts  109 us (42%)
  waiting for transfers between devices  76 us (29%)
  matrix products  36.7 us (14%)
  between operations  14.1 us (5%)
  blocking collectives  12 us (5%)
  starting transfers between devices  5.46 us (2%)
  other arithmetic  4.22 us (2%)
    gather x1, local copies, waits for them, and re-layouts, shards(): selected = jnp.take(whole, basis_map, axis=0)  106 us
    all_gather x1, waiting for transfers between devices, shards(): whole = lax.all_gather(coeffs, 'row', axis=0, tiled=True)  65.6 us
    dot_general x1, matrix products, shards(): jnp.einsum('bps,bsk->bpk', masked, selected, preferred_element_type=jnp.f...  28.6 us
    all_to_all x1, blocking collectives, sent_to_all(): return lax.all_to_all(copies, axis, split_axis=0, concat_axis=0, tiled=True)  12 us
    all_to_all x1, waiting for transfers between devices, sent_to_all(): return lax.all_to_all(copies, axis, split_axis=0, concat_axis=0, tiled=True)  9.74 us
    dot_general x1, matrix products, shards(): jnp.einsum('blp,bp->bl', harmonics, full_density, precision=lax.Precision...  7.84 us
    all_to_all x1, starting transfers between devices, sent_to_all(): return lax.all_to_all(copies, axis, split_axis=0, concat_axis=0, tiled=True)  5.42 us
  transfers between devices with their start and end apart: 2, of which 2 were waited for; matrix products, arithmetic and copies ran while one was open for 1% of the time, Pallas kernels for 0%

commit v1 on v0

v1 whole, which is shorter than its diff:
```python
import jax
import jax.numpy as jnp
from jax import lax
from jax.experimental import pallas as pl
from jax.experimental.pallas import tpu as pltpu
from jax.sharding import Mesh, PartitionSpec as P

NATOM = 64
WIN = 96
GROUPS = 8
LANES = 128


def density_kernel(idx_ref, w_ref, occ_ref, m_ref, out_ref, wide, even, odd, acc):
    step = pl.program_id(0)
    slots = m_ref.shape[2]
    stride = slots + 1
    rows = w_ref.shape[0]

    def pick(into, batch, low, high):
        for s in range(low, high):
            at = pl.multiple_of(idx_ref[batch * slots + s], GROUPS)
            into[pl.ds(s, GROUPS, stride=stride), :] = wide[pl.ds(at, GROUPS), :]

    def multiply(held, which, tile):
        right = jnp.concatenate(
            [held[pl.ds((2 * tile + h) * stride, slots), :].astype(jnp.bfloat16) for h in range(2)], axis=1
        )
        orbital = jnp.dot(m_ref[which], right, preferred_element_type=jnp.float32)
        left_half, right_half = orbital[:, :LANES], orbital[:, LANES:]
        term = (
            left_half * left_half * occ_ref[2 * tile : 2 * tile + 1, :]
            + right_half * right_half * occ_ref[2 * tile + 1 : 2 * tile + 2, :]
        )
        acc[which] = term if tile == 0 else acc[which] + term

    @pl.when(step == 0)
    def _():
        for r in range(0, rows, 512):
            wide[pl.ds(r, 512), :] = w_ref[pl.ds(r, 512), :].astype(jnp.float32)
        wide[pl.ds(rows, GROUPS), :] = jnp.zeros((GROUPS, LANES), jnp.float32)
        pick(even, 0, 0, slots)

    tiles = GROUPS // 2
    for which in range(2):
        held, into = (even, odd) if which == 0 else (odd, even)
        for tile in range(tiles):
            pick(into, 2 * step + which + 1, tile * slots // tiles, (tile + 1) * slots // tiles)
            multiply(held, which, tile)
    for which in range(2):
        out_ref[0, pl.ds(which, 1), :] = jnp.sum(acc[which].T, axis=0, keepdims=True)


def partial_densities(idx, window, occ, basis_on_grid):
    batches, points, slots = basis_on_grid.shape
    rows = window.shape[0]
    out = pl.pallas_call(
        density_kernel,
        grid=(batches // 2,),
        in_specs=[
            pl.BlockSpec(memory_space=pltpu.SMEM),
            pl.BlockSpec((rows, LANES), lambda i: (0, 0), pipeline_mode=pl.Buffered(1)),
            pl.BlockSpec((GROUPS, LANES), lambda i: (0, 0)),
            pl.BlockSpec((2, points, slots), lambda i: (i, 0, 0)),
        ],
        out_specs=pl.BlockSpec((1, 2, points), lambda i: (i, 0, 0)),
        out_shape=jax.ShapeDtypeStruct((batches // 2, 2, points), jnp.float32),
        scratch_shapes=[
            pltpu.VMEM((rows + GROUPS, LANES), jnp.float32),
            pltpu.VMEM(((slots + 1) * GROUPS + 8, LANES), jnp.float32),
            pltpu.VMEM(((slots + 1) * GROUPS + 8, LANES), jnp.float32),
            pltpu.VMEM((2, points, LANES), jnp.float32),
        ],
        compiler_params=pltpu.CompilerParams(vmem_limit_bytes=60 * 2**20),
        cost_estimate=pl.CostEstimate(
            flops=2 * batches * points * slots * GROUPS * LANES, bytes_accessed=batches * points * slots * 2, transcendentals=0
        ),
    )(idx, window, occ, basis_on_grid)
    return out.reshape(batches, points)


def shards(coeffs, occupation, basis_on_grid, basis_map, basis_count, batch_atom, harmonics):
    batches, points, slots = basis_on_grid.shape
    parity = lax.axis_index("core")
    shard = coeffs.shape[0]
    halves = coeffs.reshape(2, WIN, GROUPS, LANES)
    mine = lax.dynamic_index_in_dim(halves, parity, 0, keepdims=False)
    other = lax.dynamic_index_in_dim(halves, 1 - parity, 0, keepdims=False)
    theirs = lax.ppermute(other, "core", [(0, 1), (1, 0)])
    first = jnp.where(parity == 0, mine, theirs)
    second = jnp.where(parity == 0, theirs, mine)
    both = jnp.concatenate([first, second], axis=0).reshape(2 * WIN * GROUPS, LANES)
    window = lax.all_gather(both, "chip", axis=0, tiled=True)
    place = (basis_map // shard) * WIN + basis_map % shard - parity * WIN
    slot_ids = lax.broadcasted_iota(jnp.int32, (batches, slots), 1)
    place = jnp.where(slot_ids < basis_count[:, None], place, window.shape[0] // GROUPS) * GROUPS
    idx = jnp.concatenate([place.reshape(-1), place[0]])
    part = partial_densities(idx, window, occupation.reshape(GROUPS, LANES), basis_on_grid)
    zs = lax.axis_size("col")
    share = points // zs
    pieces = lax.all_to_all(part.reshape(batches, zs, share).transpose(1, 0, 2), "col", split_axis=0, concat_axis=0, tiled=True)
    density = jnp.sum(pieces, axis=0)
    mine_harm = lax.dynamic_slice_in_dim(harmonics, lax.axis_index("col") * share, share, 2)
    local_moment = jnp.einsum("blp,bp->bl", mine_harm, density, precision=lax.Precision.HIGHEST)
    atom_ids = lax.broadcasted_iota(jnp.int32, (batches, NATOM), 1)
    member = (batch_atom[:, None] == atom_ids).astype(jnp.float32)
    atom_part = jnp.dot(member.T, local_moment, precision=lax.Precision.HIGHEST)
    moments = lax.psum(atom_part, ("chip", "core", "col"))
    return density, moments


def solution(mesh):
    rows, cols = mesh.devices.shape
    split = Mesh(mesh.devices.reshape(rows // 2, 2, cols), ("chip", "core", "col"))
    row = ("chip", "core")
    placed = (
        P(row, "col"),
        P("col"),
        P(row, None, None),
        P(row, None),
        P(row),
        P(row),
        P(row, None, None),
    )
    return jax.shard_map(shards, mesh=split, in_specs=placed, out_specs=(P(row, "col"), P()), check_vma=False)
```

time: 259 us -> 201 us (0.78)
  local copies, waits for them, and re-layouts: 109 us -> 3.99 us
  blocking collectives: 12 us -> 63.1 us
  Pallas kernels: 0 us -> 41.3 us
  matrix products: 36.7 us -> 2.14 us
  waiting for transfers between devices: 76 us -> 67 us
    gather x1 -> x0, local copies, waits for them, and re-layouts: 106 us -> none  [shards(): selected = jnp.take(whole, basis_map, axis=0)]
    psum x0 -> x1, blocking collectives: none -> 63.1 us  [shards(): moments = lax.psum(atom_part, ('chip', 'core', 'col'))]
    pallas_call x0 -> x1, Pallas kernels: none -> 41.3 us  [partial_densities(): pl.pallas_call(density_kernel, grid=(batches // 2,), in_specs=[pl.BlockSp...]
    dot_general x2 -> x1, matrix products: 36.4 us -> 1.9 us  [shards(): jnp.einsum('blp,bp->bl', mine_harm, density, precision=lax.Precision.HIGH...]
    all_to_all x1 -> x0, blocking collectives: 12 us -> none  [sent_to_all(): return lax.all_to_all(copies, axis, split_axis=0, concat_axis=0, tiled=True)]
    all_to_all x1, waiting for transfers between devices: 9.74 us -> 4.44 us  [shards(): lax.all_to_all(part.reshape(batches, zs, share).transpose(1, 0, 2), 'col'...]
    all_gather x1, waiting for transfers between devices: 65.6 us -> 61.1 us  [shards(): window = lax.all_gather(both, 'chip', axis=0, tiled=True)]
  transfers between devices with their start and end apart: 2 -> 3, of which waited for: 2 -> 3; matrix products, arithmetic and copies ran while one was open for 1% -> 2% of each run, Pallas kernels for 0% -> 0%
where the time goes in v1:
time: 201 us; the launch traced here: 200 us
  waiting for transfers between devices  67 us (33%)
  blocking collectives  63.1 us (31%)
  Pallas kernels  41.3 us (21%)
  between operations  14.1 us (7%)
  starting transfers between devices  4.55 us (2%)
  local copies, waits for them, and re-layouts  3.99 us (2%)
  other arithmetic  3.45 us (2%)
  matrix products  2.14 us (1%)
    psum x1, blocking collectives, shards(): moments = lax.psum(atom_part, ('chip', 'core', 'col'))  63.1 us
    all_gather x1, waiting for transfers between devices, shards(): window = lax.all_gather(both, 'chip', axis=0, tiled=True)  61.1 us
    pallas_call x1, Pallas kernels, partial_densities(): pl.pallas_call(density_kernel, grid=(batches // 2,), in_specs=[pl.BlockSp...  41.3 us
    all_to_all x1, waiting for transfers between devices, shards(): lax.all_to_all(part.reshape(batches, zs, share).transpose(1, 0, 2), 'col'...  4.44 us
    all_to_all x1, starting transfers between devices, shards(): lax.all_to_all(part.reshape(batches, zs, share).transpose(1, 0, 2), 'col'...  4.43 us
  transfers between devices with their start and end apart: 3, of which 3 were waited for; matrix products, arithmetic and copies ran while one was open for 2% of the time, Pallas kernels for 0%

profile of v1, /device:TPU:0, one launch (start us, length us, event | category | flops | bytes accessed | tf_op | source)
XLA Modules:
  0.0 199.7 jit_solution(17137511968603957565)
XLA Ops:
  7.2 0.0 all-gather.2.cloned.1.call-start
  7.2 1.1 copy.14
  8.3 0.1 collective-permute-start
  8.4 1.4 collective-permute-done
  9.9 0.8 maximum_bitcast_fusion
  10.6 0.0 all-gather.2.cloned.1.call-update
  10.7 1.0 fusion.12
  11.7 1.0 fusion.6
  12.7 0.6 pad_add_fusion.idx_ref
  13.4 61.1 %all-gather.2.cloned.1.call-done.w_ref = bf16[24576,128]{1,0:T(8,128)(2,1)} async-done(((bf16[1536,128]{1,0:T(8,128)(2,1)}), bf16[24576,128]{1,0:T(8,128)(2,1)}) %all-gather.2.cloned.1.call-update) | async-done | bytes 6291472 | tf_op jit(solution)/shard_map/all_gather | solution.py:93
  74.5 0.0 copy-start.1
  74.5 41.3 %shard_map.86 = f32[20,2,512]{2,1,0:T(2,128)} custom-call(s32[20992]{0:T(1024)} %pad_add_fusion.idx_ref, bf16[24576,128]{1,0:T(8,128)(2,1)} %all-gather.2.cloned.1.call-done.w_ref, f32[8,128]{1,0:T(8,128)} %bitcast.32, bf16[40,512,512]{2,1,0:T(8,128)(2,1)} %m_ref.1), custom_call_target="tpu_custom_call" | custom-call | flops 21474836480 | bytes 20971520 | tf_op jit(solution)/shard_map/pallas_call | solution.py:57
  115.7 1.0 reshape_reshape.3
  116.7 0.6 copy.18
  117.3 4.4 %all-to-all-start = ((f32[4,40,128]{2,1,0:T(8,128)}), f32[4,40,128]{2,1,0:T(8,128)S(1)}, u32[]{:S(2)}, u32[]{:S(2)}) async-start(f32[4,40,128]{2,1,0:T(8,128)} %bitcast.24), calls=%async_computation | async-start | bytes 163840 | tf_op jit(solution)/shard_map/all_to_all | solution.py:101
  121.8 1.3 constant_dynamic-slice_fusion
  123.0 4.4 %all-to-all-done = f32[4,40,128]{2,1,0:T(8,128)S(1)} async-done(((f32[4,40,128]{2,1,0:T(8,128)}), f32[4,40,128]{2,1,0:T(8,128)S(1)}, u32[]{:S(2)}, u32[]{:S(2)}) %all-to-all-start) | async-done | bytes 81952 | tf_op jit(solution)/shard_map/all_to_all | solution.py:101
  127.5 0.0 copy-start
  127.5 1.9 fusion
  129.4 0.0 copy-done.1
  129.4 0.2 fusion.8
  129.7 63.1 %psum.7 = f32[64,49]{0,1:T(8,128)} all-reduce(f32[64,49]{0,1:T(8,128)S(1)} %fusion.8), channel_id=1, replica_groups=mesh['chip'=16,'core'=2,'col'=4] {'chip','core','col'}, use_global_device_ids=true, to_apply=%region_1.2 | all-reduce | flops 3136 | bytes 25088 | tf_op jit(solution)/shard_map/psum | solution.py:108
  192.8 0.0 copy-done
  (5 shorter events, 0.1 us)
Async XLA Ops:
  7.2 67.3 %all-gather.2.cloned.1.call-start = ((), (), s32[]{:S(2)}) async-start(), calls=%async_computation.1 | async-start | bytes 6684672 | tf_op jit(solution)/shard_map/all_gather | solution.py:93
  8.3 1.5 collective-permute-start
  74.5 54.9 %copy-start.1 = (s32[40]{0:T(128)S(1)}, s32[40]{0:T(128)}, u32[]{:S(2)}) copy-start(s32[40]{0:T(128)} %param.12) | copy-start | bytes 484
  117.3 10.1 %all-to-all-start = ((f32[4,40,128]{2,1,0:T(8,128)}), f32[4,40,128]{2,1,0:T(8,128)S(1)}, u32[]{:S(2)}, u32[]{:S(2)}) async-start(f32[4,40,128]{2,1,0:T(8,128)} %bitcast.24), calls=%async_computation | async-start | bytes 163840 | tf_op jit(solution)/shard_map/all_to_all | solution.py:101
  127.5 65.3 %copy-start = (f32[40,128]{1,0:T(8,128)}, f32[40,128]{1,0:T(8,128)S(1)}, u32[]{:S(2)}) copy-start(f32[40,128]{1,0:T(8,128)S(1)} %reduce_sum.9) | copy-start | bytes 61444
Sparse Core Ops, SparseCore 0:
  10.8 63.6 all-gather.1

commit v2 on v1

v2 whole, which is shorter than its diff:
```python
import jax
import jax.numpy as jnp
from jax import lax
from jax.experimental import pallas as pl
from jax.experimental.pallas import tpu as pltpu
from jax.sharding import PartitionSpec as P

NATOM = 64
SIDE = 4
MESH = pl.DeviceIdType.MESH
WIN = 96
GROUPS = 8
LANES = 128


def place_of(row):
    return row // (2 * SIDE), (row // 2) % SIDE, row % 2


def window_kernel(coeffs_ref, out_ref, staged, other, send_sem, recv_sem):
    me = lax.axis_index("row")
    col = lax.axis_index("col")
    y, x, core = place_of(me)
    block = WIN * GROUPS

    def row_of(dy, dx):
        return (lax.rem(y + dy + SIDE, SIDE) * SIDE + lax.rem(x + dx + SIDE, SIDE)) * 2 + core

    def turned(first, second, turn):
        return first * turn + second * (1 - turn), first * (1 - turn) + second * turn

    def rows_of(first, second, turn, half):
        q = row_of(*turned(first, second, turn)) - core + turn
        if half is None:
            return pl.ds(pl.multiple_of(q * block, block), block)
        return pl.ds(pl.multiple_of(q * block + half * (block // 2), block // 2), block // 2)

    def copy(turn, number, at, to, half=None):
        here = out_ref.at[rows_of(*at, turn, half)]
        sem = turn * 20 + number
        return pltpu.make_async_remote_copy(
            src_ref=here, dst_ref=here, send_sem=send_sem.at[sem], recv_sem=recv_sem.at[sem],
            device_id=(row_of(*turned(*to, turn)), col), device_id_type=MESH,
        )

    sent = []

    def send(turn, number, at, to, half=None):
        one = copy(turn, number, at, to, half)
        one.start()
        sent.append(one)

    def arrive(turn, number, at, half=None):
        copy(turn, number, at, (0, 1), half).wait_recv()

    for j in range(GROUPS):
        staged[pl.ds(j, 2 * WIN, stride=GROUPS), :] = coeffs_ref[:, j * LANES : (j + 1) * LANES].astype(jnp.float32)
    mine = pl.multiple_of(core * block, block)
    theirs = pl.multiple_of((1 - core) * block, block)
    other[...] = staged[pl.ds(theirs, block), :].astype(jnp.bfloat16)
    own_rows = rows_of(0, 0, core, None)
    out_ref[own_rows, :] = staged[pl.ds(mine, block), :].astype(jnp.bfloat16)

    barrier = pltpu.get_barrier_semaphore()
    partner = me - core + (1 - core)
    near = [partner, row_of(0, 1), row_of(0, -1), row_of(1, 0), row_of(-1, 0)]
    for row in near:
        pl.semaphore_signal(barrier, inc=1, device_id=(row, col), device_id_type=MESH)
    pl.semaphore_wait(barrier, len(near))

    swap = pltpu.make_async_remote_copy(
        src_ref=other, dst_ref=out_ref.at[own_rows], send_sem=send_sem.at[40], recv_sem=recv_sem.at[40],
        device_id=(partner, col), device_id_type=MESH,
    )
    swap.start()
    a, b = core, 1 - core
    blocks = [(0, 0), (-1, 0), (1, 0), (2, 0)]

    def outward(turn):
        send(turn, 0, (0, 0), (1, 0))
        send(turn, 1, (0, 0), (-1, 0))
        across(turn, 0)

    def across(turn, k):
        send(turn, 4 + 2 * k, blocks[k], (0, 1))
        send(turn, 5 + 2 * k, blocks[k], (0, -1))

    def first_hop(turn):
        arrive(turn, 0, (-1, 0))
        send(turn, 2, (-1, 0), (1, 0), 0)
        arrive(turn, 1, (1, 0))
        send(turn, 3, (1, 0), (-1, 0), 1)
        across(turn, 1)
        across(turn, 2)

    def second_hop(turn):
        arrive(turn, 2, (2, 0), 0)
        arrive(turn, 3, (2, 0), 1)
        across(turn, 3)

    def onward(turn, k):
        f = blocks[k][0]
        arrive(turn, 4 + 2 * k, (f, -1))
        send(turn, 12 + 2 * k, (f, -1), (0, 1), 0)
        arrive(turn, 5 + 2 * k, (f, 1))
        send(turn, 13 + 2 * k, (f, 1), (0, -1), 1)

    outward(a)
    pltpu.make_async_remote_copy(
        src_ref=other, dst_ref=out_ref.at[rows_of(0, 0, b, None)], send_sem=send_sem.at[40], recv_sem=recv_sem.at[40],
        device_id=(partner, col), device_id_type=MESH,
    ).wait_recv()
    outward(b)
    first_hop(a)
    onward(a, 0)
    first_hop(b)
    onward(b, 0)
    second_hop(a)
    second_hop(b)
    for k in (1, 2, 3):
        onward(a, k)
        onward(b, k)
    for turn in (a, b):
        for k in range(4):
            f = blocks[k][0]
            arrive(turn, 12 + 2 * k, (f, 2), 0)
            arrive(turn, 13 + 2 * k, (f, 2), 1)
    swap.wait_send()
    for one in sent:
        one.wait_send()


def gather_window(coeffs):
    rows = 2 * SIDE * SIDE * WIN * GROUPS
    return pl.pallas_call(
        window_kernel,
        out_shape=jax.ShapeDtypeStruct((rows, LANES), jnp.bfloat16),
        in_specs=[pl.BlockSpec(memory_space=pltpu.VMEM)],
        out_specs=pl.BlockSpec(memory_space=pltpu.VMEM),
        scratch_shapes=[
            pltpu.VMEM((2 * WIN * GROUPS, LANES), jnp.float32),
            pltpu.VMEM((WIN * GROUPS, LANES), jnp.bfloat16),
            pltpu.SemaphoreType.DMA((41,)),
            pltpu.SemaphoreType.DMA((41,)),
        ],
        compiler_params=pltpu.CompilerParams(collective_id=0, has_side_effects=True, vmem_limit_bytes=16 * 2**20),
    )(coeffs)


def total_kernel(part_ref, atoms_ref, density_ref, moments_ref, parts, column, line, plane, square, send_sem, recv_sem):
    me = lax.axis_index("row")
    z = lax.axis_index("col")
    y, x, core = place_of(me)
    pairs = [(dz, dc) for dz in range(SIDE) for dc in range(2) if (dz, dc) != (0, 0)]

    def column_device(dz, dc):
        return me - core + lax.rem(core + dc, 2), lax.rem(z + dz, SIDE)

    def line_device(d):
        return (y * SIDE + lax.rem(x + d, SIDE)) * 2 + core, z

    def plane_device(d):
        return (lax.rem(y + d, SIDE) * SIDE + x) * 2 + core, z

    barrier = pltpu.get_barrier_semaphore()
    near = [column_device(*p) for p in pairs] + [line_device(d) for d in (1, 2, 3)] + [plane_device(d) for d in (1, 2, 3)]
    for device in near:
        pl.semaphore_signal(barrier, inc=1, device_id=device, device_id_type=MESH)
    pl.semaphore_wait(barrier, len(near))

    def remote(src, dst, number, device):
        return pltpu.make_async_remote_copy(
            src_ref=src, dst_ref=dst, send_sem=send_sem.at[number], recv_sem=recv_sem.at[number],
            device_id=device, device_id_type=MESH,
        )

    slot = z * 2 + core
    sends = []
    for n, (dz, dc) in enumerate(pairs):
        sends.append(remote(atoms_ref, column.at[slot], n, column_device(dz, dc)))
    for dz in (1, 2, 3):
        sends.append(remote(part_ref.at[lax.rem(z + dz, SIDE)], parts.at[z], 6 + dz, column_device(dz, 0)))
    for one in sends:
        one.start()
    column[slot] = atoms_ref[...]
    parts[z] = part_ref[z]
    for n, (dz, dc) in enumerate(pairs):
        source = lax.rem(z - dz + SIDE, SIDE) * 2 + lax.rem(core + dc, 2)
        remote(atoms_ref, column.at[source], n, column_device(dz, dc)).wait_recv()
    here = column[0]
    for s in range(1, 2 * SIDE):
        here = here + column[s]
    line[x] = here
    lines = [remote(line.at[x], line.at[x], 9 + d, line_device(d)) for d in (1, 2, 3)]
    for one in lines:
        one.start()
    for dz in (1, 2, 3):
        source = lax.rem(z - dz + SIDE, SIDE)
        remote(part_ref.at[0], parts.at[source], 6 + dz, column_device(dz, 0)).wait_recv()
    density_ref[...] = parts[0] + parts[1] + parts[2] + parts[3]
    for d in (1, 2, 3):
        source = lax.rem(x - d + SIDE, SIDE)
        remote(line.at[source], line.at[source], 9 + d, line_device(d)).wait_recv()
    plane[y] = line[0] + line[1] + line[2] + line[3]
    planes = [remote(plane.at[y], plane.at[y], 12 + d, plane_device(d)) for d in (1, 2, 3)]
    for one in planes:
        one.start()
    for d in (1, 2, 3):
        source = lax.rem(y - d + SIDE, SIDE)
        remote(plane.at[source], plane.at[source], 12 + d, plane_device(d)).wait_recv()
    square[...] = jnp.zeros_like(square)
    square[pl.ds(0, plane.shape[1]), :] = plane[0] + plane[1] + plane[2] + plane[3]
    moments_ref[...] = square[...].T[: moments_ref.shape[0], : moments_ref.shape[1]]
    for one in sends + lines + planes:
        one.wait_send()


def totals(part, atoms, components):
    zs, batches, share = part.shape
    kept = atoms.shape[0]
    return pl.pallas_call(
        total_kernel,
        out_shape=(
            jax.ShapeDtypeStruct((batches, share), jnp.float32),
            jax.ShapeDtypeStruct((NATOM, components), jnp.float32),
        ),
        in_specs=[pl.BlockSpec(memory_space=pltpu.VMEM)] * 2,
        out_specs=(pl.BlockSpec(memory_space=pltpu.VMEM), pl.BlockSpec(memory_space=pltpu.VMEM)),
        scratch_shapes=[
            pltpu.VMEM((zs, batches, share), jnp.float32),
            pltpu.VMEM((2 * SIDE, kept, LANES), jnp.float32),
            pltpu.VMEM((SIDE, kept, LANES), jnp.float32),
            pltpu.VMEM((SIDE, kept, LANES), jnp.float32),
            pltpu.VMEM((LANES, LANES), jnp.float32),
            pltpu.SemaphoreType.DMA((16,)),
            pltpu.SemaphoreType.DMA((16,)),
        ],
        compiler_params=pltpu.CompilerParams(collective_id=1, has_side_effects=True, vmem_limit_bytes=16 * 2**20),
    )(part, atoms)


def density_kernel(idx_ref, atom_ref, w_ref, occ_ref, m_ref, harm_ref, out_ref, sums_ref, wide, even, odd, acc):
    step = pl.program_id(0)
    slots = m_ref.shape[2]
    stride = slots + 1
    rows = w_ref.shape[0]

    def pick(into, batch, low, high):
        for s in range(low, high):
            at = pl.multiple_of(idx_ref[batch * slots + s], GROUPS)
            into[pl.ds(s, GROUPS, stride=stride), :] = wide[pl.ds(at, GROUPS), :]

    def multiply(held, which, tile):
        right = jnp.concatenate(
            [held[pl.ds((2 * tile + h) * stride, slots), :].astype(jnp.bfloat16) for h in range(2)], axis=1
        )
        orbital = jnp.dot(m_ref[which], right, preferred_element_type=jnp.float32)
        left_half, right_half = orbital[:, :LANES], orbital[:, LANES:]
        term = (
            left_half * left_half * occ_ref[2 * tile : 2 * tile + 1, :]
            + right_half * right_half * occ_ref[2 * tile + 1 : 2 * tile + 2, :]
        )
        acc[which] = term if tile == 0 else acc[which] + term

    @pl.when(step == 0)
    def _():
        for r in range(0, rows, 512):
            wide[pl.ds(r, 512), :] = w_ref[pl.ds(r, 512), :].astype(jnp.float32)
        wide[pl.ds(rows, GROUPS), :] = jnp.zeros((GROUPS, LANES), jnp.float32)
        sums_ref[...] = jnp.zeros_like(sums_ref)
        pick(even, 0, 0, slots)

    tiles = GROUPS // 2
    for which in range(2):
        held, into = (even, odd) if which == 0 else (odd, even)
        for tile in range(tiles):
            pick(into, 2 * step + which + 1, tile * slots // tiles, (tile + 1) * slots // tiles)
            multiply(held, which, tile)
    atom_ids = lax.broadcasted_iota(jnp.int32, (harm_ref.shape[1], LANES), 1)
    for which in range(2):
        row = jnp.sum(acc[which].T, axis=0, keepdims=True)
        for z in range(out_ref.shape[0]):
            out_ref[z, pl.ds(2 * step + which, 1), :] = row[:, z * LANES : (z + 1) * LANES]
        moment = jnp.sum(harm_ref[which] * row, axis=1, keepdims=True)
        mine = atom_ids == atom_ref[2 * step + which]
        sums_ref[pl.ds(0, harm_ref.shape[1]), :] += jnp.where(mine, moment, 0.0)


def partial_densities(idx, batch_atom, window, occ, basis_on_grid, harmonics):
    batches, points, slots = basis_on_grid.shape
    rows = window.shape[0]
    components = harmonics.shape[1]
    kept = -(-components // 8) * 8
    return pl.pallas_call(
        density_kernel,
        grid=(batches // 2,),
        in_specs=[
            pl.BlockSpec(memory_space=pltpu.SMEM),
            pl.BlockSpec(memory_space=pltpu.SMEM),
            pl.BlockSpec((rows, LANES), lambda i: (0, 0), pipeline_mode=pl.Buffered(1)),
            pl.BlockSpec((GROUPS, LANES), lambda i: (0, 0)),
            pl.BlockSpec((2, points, slots), lambda i: (i, 0, 0)),
            pl.BlockSpec((2, components, points), lambda i: (i, 0, 0)),
        ],
        out_specs=(
            pl.BlockSpec((points // LANES, batches, LANES), lambda i: (0, 0, 0)),
            pl.BlockSpec((kept, LANES), lambda i: (0, 0)),
        ),
        out_shape=(
            jax.ShapeDtypeStruct((points // LANES, batches, LANES), jnp.float32),
            jax.ShapeDtypeStruct((kept, LANES), jnp.float32),
        ),
        scratch_shapes=[
            pltpu.VMEM((rows + GROUPS, LANES), jnp.float32),
            pltpu.VMEM(((slots + 1) * GROUPS + 8, LANES), jnp.float32),
            pltpu.VMEM(((slots + 1) * GROUPS + 8, LANES), jnp.float32),
            pltpu.VMEM((2, points, LANES), jnp.float32),
        ],
        compiler_params=pltpu.CompilerParams(vmem_limit_bytes=60 * 2**20),
        cost_estimate=pl.CostEstimate(
            flops=2 * batches * points * slots * GROUPS * LANES, bytes_accessed=batches * points * slots * 2, transcendentals=0
        ),
    )(idx, batch_atom, window, occ, basis_on_grid, harmonics)


def shards(coeffs, occupation, basis_on_grid, basis_map, basis_count, batch_atom, harmonics):
    batches, points, slots = basis_on_grid.shape
    parity = lax.rem(lax.axis_index("row"), 2)
    shard = coeffs.shape[0]
    window = gather_window(coeffs)
    place = (basis_map // shard) * WIN + basis_map % shard - parity * WIN
    slot_ids = lax.broadcasted_iota(jnp.int32, (batches, slots), 1)
    place = jnp.where(slot_ids < basis_count[:, None], place, window.shape[0] // GROUPS) * GROUPS
    idx = jnp.concatenate([place.reshape(-1), place[0]])
    part, atoms = partial_densities(
        idx, batch_atom, window, occupation.reshape(GROUPS, LANES), basis_on_grid, harmonics
    )
    return totals(part, atoms, harmonics.shape[1])


def solution(mesh):
    placed = (
        P("row", "col"),
        P("col"),
        P("row", None, None),
        P("row", None),
        P("row"),
        P("row"),
        P("row", None, None),
    )
    return jax.shard_map(shards, mesh=mesh, in_specs=placed, out_specs=(P("row", "col"), P()), check_vma=False)
```

time: 201 us -> 116 us (0.58)
  waiting for transfers between devices: 67 us -> 0 us
  blocking collectives: 63.1 us -> 0 us
  Pallas kernels: 41.3 us -> 99.7 us
  between operations: 14.1 us -> 0.69 us
  local copies, waits for them, and re-layouts: 3.99 us -> 12.3 us
  starting transfers between devices: 4.55 us -> 0 us
  matrix products: 2.14 us -> 0 us
    psum x1 -> x0, blocking collectives: 63.1 us -> none  [shards(): moments = lax.psum(atom_part, ('chip', 'core', 'col'))]
    all_gather x1 -> x0, waiting for transfers between devices: 61.1 us -> none  [shards(): window = lax.all_gather(both, 'chip', axis=0, tiled=True)]
    pallas_call x0 -> x2, Pallas kernels: none -> 57.1 us  [the longest x1 39.2 us: gather_window(): pl.pallas_call(window_kernel, out_shape=jax.ShapeDtypeStruct((rows, LANES...]
    unnamed x6 -> x11, local copies, waits for them, and re-layouts: 1.09 us -> 11.6 us
    all_to_all x1 -> x0, waiting for transfers between devices: 4.44 us -> none  [shards(): lax.all_to_all(part.reshape(batches, zs, share).transpose(1, 0, 2), 'col'...]
    all_to_all x1 -> x0, starting transfers between devices: 4.43 us -> none  [shards(): lax.all_to_all(part.reshape(batches, zs, share).transpose(1, 0, 2), 'col'...]
    dot_general x2 -> x0, matrix products: 2.14 us -> none  [the longest x1 1.9 us: shards(): jnp.einsum('blp,bp->bl', mine_harm, density, precision=lax.Precision.HIGH...]
  transfers between devices with their start and end apart: 3 -> 0, of which waited for: 3 -> 0; matrix products, arithmetic and copies ran while one was open for 2% -> 0% of each run, Pallas kernels for 0% -> 0%
where the time goes in v2:
time: 116 us; the launch traced here: 115 us
  Pallas kernels  99.7 us (86%)
  local copies, waits for them, and re-layouts  12.3 us (11%)
  other arithmetic  2.67 us (2%)
    pallas_call x1, Pallas kernels, partial_densities(): pl.pallas_call(density_kernel, grid=(batches // 2,), in_specs=[pl.BlockSp...  42.6 us
    pallas_call x1, Pallas kernels, gather_window(): pl.pallas_call(window_kernel, out_shape=jax.ShapeDtypeStruct((rows, LANES...  39.2 us
    pallas_call x1, Pallas kernels, totals(): pl.pallas_call(total_kernel, out_shape=(jax.ShapeDtypeStruct((batches, sh...  17.9 us
    unnamed x11, local copies, waits for them, and re-layouts  11.6 us

profile of v2, /device:TPU:0, one launch (start us, length us, event | category | flops | bytes accessed | tf_op | source)
XLA Modules:
  0.0 115.3 jit_solution(7214287289137495954)
XLA Ops:
  0.6 0.0 copy-start.1
  0.6 1.0 fusion.6
  1.7 1.0 fusion.4
  2.7 0.6 pad_add_fusion.idx_ref
  3.4 6.7 %copy.9.harm_ref = f32[40,49,512]{2,1,0:T(8,128)} copy(f32[40,49,512]{2,0,1:T(8,128)} %param.13) | data formatting | bytes 8028160 | tf_op args[6]
  10.0 0.0 copy-done.1
  10.0 39.2 %shard_map.86.w_ref = bf16[24576,128]{1,0:T(8,128)(2,1)S(1)} custom-call(bf16[192,1024]{1,0:T(8,128)(2,1)S(1)} %copy-done.1), custom_call_target="tpu_custom_call" | custom-call | tf_op jit(solution)/shard_map/pallas_call | solution.py:135
  49.3 0.0 copy-start
  49.3 2.6 %copy-done = bf16[24576,128]{1,0:T(8,128)(2,1)} copy-done((bf16[24576,128]{1,0:T(8,128)(2,1)}, bf16[24576,128]{1,0:T(8,128)(2,1)S(1)}, u32[]{:S(2)}) %copy-start) | copy-done | bytes 6291480
  51.9 42.6 %shard_map.87 = (f32[4,40,128]{2,1,0:T(8,128)}, f32[56,128]{1,0:T(8,128)}) custom-call(s32[20992]{0:T(1024)} %pad_add_fusion.idx_ref, s32[40]{0:T(128)} %atom_ref.1, bf16[24576,128]{1,0:T(8,128)(2,1)} %copy-done, f32[8,128]{1,0:T(8,128)} %bitcast.7, bf16[40,512,512]{2,1,0:T(8,128)(2,1)} %m_ref.1, f32[40,49,512]{2,1,0:T(8,128)} %copy.9.harm_ref), custom_call_target="tpu_custom_call" | custom-call | flops 21474836480 | bytes 20971520 | tf_op jit(solution)/shard_map/pallas_call | solution.py:294
  94.5 0.0 copy-start.2
  94.5 0.9 copy-done.2
  95.4 0.0 copy-start.3
  95.4 0.7 copy-done.3
  96.1 17.9 %shard_map.88 = (f32[40,128]{1,0:T(8,128)S(1)}, f32[64,49]{1,0:T(8,128)S(1)}) custom-call(f32[4,40,128]{2,1,0:T(8,128)S(1)} %copy-done.2, f32[56,128]{1,0:T(8,128)S(1)} %copy-done.3), custom_call_target="tpu_custom_call" | custom-call | tf_op jit(solution)/shard_map/pallas_call | solution.py:221
  114.0 0.7 copy.10
  114.7 0.6 copy.13
  (2 shorter events, 0.0 us)
Async XLA Ops:
  0.6 9.4 %copy-start.1 = (bf16[192,1024]{1,0:T(8,128)(2,1)S(1)}, bf16[192,1024]{1,0:T(8,128)(2,1)}, u32[]{:S(2)}) copy-start(bf16[192,1024]{1,0:T(8,128)(2,1)} %coeffs_ref.1) | copy-start | bytes 1179652
  49.3 2.6 %copy-start = (bf16[24576,128]{1,0:T(8,128)(2,1)}, bf16[24576,128]{1,0:T(8,128)(2,1)S(1)}, u32[]{:S(2)}) copy-start(bf16[24576,128]{1,0:T(8,128)(2,1)S(1)} %shard_map.86.w_ref) | copy-start | bytes 18874372
  94.5 0.9 copy-start.2
  95.4 0.7 copy-start.3

commit v3 on v0

v3 whole, which is shorter than its diff:
```python
import jax
import jax.numpy as jnp
from jax import lax
from jax.experimental import pallas as pl
from jax.experimental.pallas import tpu as pltpu
from jax.sharding import PartitionSpec as P

NATOM = 64
WIN = 96
LANES = 128
SIDE = 4
PASSES = 2
GROUPS = 4
BLOCK = WIN * GROUPS
UNROLL = 4
MESH = pl.DeviceIdType.MESH
OFFSETS = ((0, 0), (-1, 0), (1, 0), (2, 0))
MESSAGES = 20


def message(number):
    if number < 2:
        return (0, 0), (1 - 2 * number, 0), None
    if number < 4:
        return (2 * number - 5, 0), (5 - 2 * number, 0), number - 2
    k, down = (number - 4) // 2 % 4, number % 2
    if number < 12:
        return OFFSETS[k], (0, 1 - 2 * down), None
    return (OFFSETS[k][0], 2 * down - 1), (0, 1 - 2 * down), down


def arrival(number):
    at, to, half = message(number)
    first, second = at[0] - to[0], at[1] - to[1]
    return (2 if first == -2 else first, 2 if second == -2 else second), half


def kernel(
    idx_ref, coeffs_ref, occ_ref, m_ref, harm_hbm, member_ref, density_ref, moments_ref,
    window, staged, other, wide, even, odd, acc, harm, part, parts, column, line, plane,
    send_sem, recv_sem, sum_send, sum_recv, harm_sem,
):
    half_of_states, step = pl.program_id(0), pl.program_id(1)
    steps = pl.num_programs(1)
    me = lax.axis_index("row")
    z = lax.axis_index("col")
    y, x, core = me // (2 * SIDE), (me // 2) % SIDE, me % 2
    slots = m_ref.shape[2]
    rows = window.shape[1]

    def row_of(dy, dx):
        return (lax.rem(y + dy + SIDE, SIDE) * SIDE + lax.rem(x + dx + SIDE, SIDE)) * 2 + core

    def turned(first, second, turn):
        return first * turn + second * (1 - turn), first * (1 - turn) + second * turn

    def rows_at(at, turn, half):
        q = row_of(*turned(*at, turn)) - core + turn
        if half is None:
            return pl.ds(pl.multiple_of(q * BLOCK, BLOCK), BLOCK)
        return pl.ds(pl.multiple_of(q * BLOCK + half * (BLOCK // 2), BLOCK // 2), BLOCK // 2)

    def copy(chunk, turn, number, at, half):
        to = message(number)[1]
        place = window.at[chunk, rows_at(at, turn, half)]
        sem = chunk * 2 * MESSAGES + turn * MESSAGES + number
        return pltpu.make_async_remote_copy(
            src_ref=place, dst_ref=place, send_sem=send_sem.at[sem], recv_sem=recv_sem.at[sem],
            device_id=(row_of(*turned(*to, turn)), z), device_id_type=MESH,
        )

    def outgoing(chunk, turn, number):
        at, _, half = message(number)
        return copy(chunk, turn, number, at, half)

    def send(chunk, turn, *numbers):
        for number in numbers:
            outgoing(chunk, turn, number).start()

    def arrive(chunk, turn, *numbers):
        for number in numbers:
            at, half = arrival(number)
            copy(chunk, turn, number, at, half).wait_recv()

    a, b = core, 1 - core
    partner = me - core + b

    def swap(chunk, turn):
        sem = PASSES * 2 * MESSAGES + chunk
        return pltpu.make_async_remote_copy(
            src_ref=other.at[chunk], dst_ref=window.at[chunk, rows_at((0, 0), turn, None)],
            send_sem=send_sem.at[sem], recv_sem=recv_sem.at[sem], device_id=(partner, z), device_id_type=MESH,
        )

    def outward(chunk, turn):
        send(chunk, turn, 0, 1, 4, 5)

    def first_hop(chunk, turn):
        arrive(chunk, turn, 0)
        send(chunk, turn, 2)
        arrive(chunk, turn, 1)
        send(chunk, turn, 3, 6, 7, 8, 9)

    def second_hop(chunk, turn):
        arrive(chunk, turn, 2, 3)
        send(chunk, turn, 10, 11)

    def onward(chunk, turn, k):
        arrive(chunk, turn, 4 + 2 * k)
        send(chunk, turn, 12 + 2 * k)
        arrive(chunk, turn, 5 + 2 * k)
        send(chunk, turn, 13 + 2 * k)

    def last_arrivals(chunk):
        for turn in (a, b):
            arrive(chunk, turn, *range(12, 20))

    pairs = [(dz, dc) for dz in range(SIDE) for dc in range(2) if (dz, dc) != (0, 0)]

    def column_device(dz, dc):
        return me - core + lax.rem(core + dc, 2), lax.rem(z + dz, SIDE)

    def pick(into, batch, low, high):
        for s in range(low, high):
            into[pl.ds(s * GROUPS, GROUPS), :] = wide[pl.ds(idx_ref[batch * slots + s], GROUPS), :]

    harm_copy = pltpu.make_async_copy(harm_hbm, harm, harm_sem)

    @pl.when((half_of_states == 0) & (step == 0))
    def _():
        harm_copy.start()
        for chunk in range(PASSES):
            for j in range(GROUPS):
                lane = (chunk * GROUPS + j) * LANES
                staged[pl.ds(chunk * 2 * BLOCK + j, 2 * WIN, stride=GROUPS), :] = coeffs_ref[
                    :, lane : lane + LANES
                ].astype(jnp.float32)
            base = chunk * 2 * BLOCK
            other[chunk] = staged[pl.ds(pl.multiple_of(base + b * BLOCK, BLOCK), BLOCK), :].astype(jnp.bfloat16)
            window[chunk, rows_at((0, 0), a, None), :] = staged[
                pl.ds(pl.multiple_of(base + a * BLOCK, BLOCK), BLOCK), :
            ].astype(jnp.bfloat16)
        barrier = pltpu.get_barrier_semaphore()
        near = [column_device(*p) for p in pairs]
        near += [(row_of(0, d), z) for d in (1, 2, 3)] + [(row_of(d, 0), z) for d in (1, 2, 3)]
        for device in near:
            pl.semaphore_signal(barrier, inc=1, device_id=device, device_id_type=MESH)
        pl.semaphore_wait(barrier, len(near))
        swap(0, a).start()
        swap(1, a).start()
        outward(0, a)
        swap(0, b).wait_recv()
        outward(0, b)
        for turn in (a, b):
            first_hop(0, turn)
            onward(0, turn, 0)
        for turn in (a, b):
            second_hop(0, turn)
        for k in (1, 2, 3):
            for turn in (a, b):
                onward(0, turn, k)
        swap(1, b).wait_recv()
        outward(1, a)
        outward(1, b)
        last_arrivals(0)
        part[...] = jnp.zeros_like(part)
        wide[pl.ds(rows, 8), :] = jnp.zeros((8, LANES), jnp.float32)

    @pl.when((half_of_states == 1) & (step == 0))
    def _():
        last_arrivals(1)

    @pl.when(step == 0)
    def _():
        for r in range(0, rows, 512):
            wide[pl.ds(r, 512), :] = window[half_of_states, pl.ds(r, 512), :].astype(jnp.float32)
        pick(even, 0, 0, slots)

    @pl.when(half_of_states == 0)
    def _():
        @pl.when(step == 0)
        def _():
            first_hop(1, a)
            onward(1, a, 0)

        @pl.when(step == 1)
        def _():
            first_hop(1, b)
            onward(1, b, 0)

        @pl.when(step == 2)
        def _():
            second_hop(1, a)
            second_hop(1, b)

        for k in (1, 2, 3):
            @pl.when(step == 2 + k)
            def _():
                onward(1, a, k)
                onward(1, b, k)

    for which in range(UNROLL):
        held, into = (even, odd) if which % 2 == 0 else (odd, even)
        batch = UNROLL * step + which
        pick(into, batch + 1, 0, slots)
        right = jnp.concatenate(
            [held[pl.ds(j, slots, stride=GROUPS), :].astype(jnp.bfloat16) for j in range(GROUPS)], axis=1
        )
        orbital = jnp.dot(m_ref[which], right, preferred_element_type=jnp.float32)
        total = None
        for j in range(GROUPS):
            one = orbital[:, j * LANES : (j + 1) * LANES]
            term = one * one * occ_ref[0, j : j + 1, :]
            total = term if total is None else total + term
        acc[which] = total
        row = jnp.sum(acc[which].T, axis=0, keepdims=True)
        for c in range(SIDE):
            part[c, pl.ds(batch, 1), :] += row[:, c * LANES : (c + 1) * LANES]

    @pl.when((half_of_states == 1) & (step == steps - 1))
    def _():
        def remote(ref, slot, source, number, device):
            return pltpu.make_async_remote_copy(
                src_ref=source, dst_ref=ref.at[slot], send_sem=sum_send.at[number], recv_sem=sum_recv.at[number],
                device_id=device, device_id_type=MESH,
            )

        densities = [
            remote(parts, z, part.at[lax.rem(z + dz, SIDE)], 6 + dz, column_device(dz, 0)) for dz in (1, 2, 3)
        ]
        for one in densities:
            one.start()
        parts[z] = part[z]
        harm_copy.wait()
        lane = lax.broadcasted_iota(jnp.int32, (part.shape[1], LANES), 1)
        local = jnp.zeros((part.shape[1], LANES), jnp.float32)
        for l in range(harm.shape[0]):
            product = harm[l, :, :LANES] * part[0]
            for c in range(1, SIDE):
                product += harm[l, :, c * LANES : (c + 1) * LANES] * part[c]
            local = jnp.where(lane == l, jnp.sum(product, axis=1, keepdims=True), local)
        slot = z * 2 + core
        column[slot] = jnp.dot(
            member_ref[...], local, precision=lax.Precision.HIGHEST, preferred_element_type=jnp.float32
        )
        columns = [remote(column, slot, column.at[slot], n, column_device(*p)) for n, p in enumerate(pairs)]
        for one in columns:
            one.start()
        for dz in (1, 2, 3):
            source = lax.rem(z - dz + SIDE, SIDE)
            remote(parts, source, part.at[0], 6 + dz, column_device(dz, 0)).wait_recv()
        density_ref[...] = parts[0] + parts[1] + parts[2] + parts[3]
        for n, (dz, dc) in enumerate(pairs):
            source = lax.rem(z - dz + SIDE, SIDE) * 2 + lax.rem(core + dc, 2)
            remote(column, source, column.at[source], n, column_device(dz, dc)).wait_recv()
        here = column[0]
        for s in range(1, 2 * SIDE):
            here = here + column[s]
        line[x] = here
        lines = [remote(line, x, line.at[x], 9 + d, (row_of(0, d), z)) for d in (1, 2, 3)]
        for one in lines:
            one.start()
        for d in (1, 2, 3):
            source = lax.rem(x - d + SIDE, SIDE)
            remote(line, source, line.at[source], 9 + d, (row_of(0, d), z)).wait_recv()
        plane[y] = line[0] + line[1] + line[2] + line[3]
        planes = [remote(plane, y, plane.at[y], 12 + d, (row_of(d, 0), z)) for d in (1, 2, 3)]
        for one in planes:
            one.start()
        for d in (1, 2, 3):
            source = lax.rem(y - d + SIDE, SIDE)
            remote(plane, source, plane.at[source], 12 + d, (row_of(d, 0), z)).wait_recv()
        everything = plane[0] + plane[1] + plane[2] + plane[3]
        moments_ref[...] = everything.T[: moments_ref.shape[0], :]
        for one in densities + columns + lines + planes:
            one.wait_send()
        for chunk in range(PASSES):
            swap(chunk, a).wait_send()
            for turn in (a, b):
                for number in range(MESSAGES):
                    outgoing(chunk, turn, number).wait_send()


def shards(coeffs, occupation, basis_on_grid, basis_map, basis_count, batch_atom, harmonics):
    batches, points, slots = basis_on_grid.shape
    components = harmonics.shape[1]
    parity = lax.rem(lax.axis_index("row"), 2)
    shard = coeffs.shape[0]
    rows = 2 * SIDE * SIDE * BLOCK
    place = (basis_map // shard) * WIN + basis_map % shard - parity * WIN
    slot_ids = lax.broadcasted_iota(jnp.int32, (batches, slots), 1)
    place = jnp.where(slot_ids < basis_count[:, None], place * GROUPS, rows)
    idx = jnp.concatenate([place.reshape(-1), place[0]])
    member = (lax.broadcasted_iota(jnp.int32, (NATOM, batches), 0) == batch_atom[None, :]).astype(jnp.float32)
    density, moments = pl.pallas_call(
        kernel,
        grid=(PASSES, batches // UNROLL),
        in_specs=[
            pl.BlockSpec(memory_space=pltpu.SMEM),
            pl.BlockSpec(coeffs.shape, lambda p, i: (0, 0)),
            pl.BlockSpec((1, GROUPS, LANES), lambda p, i: (p, 0, 0)),
            pl.BlockSpec((UNROLL, points, slots), lambda p, i: (i, 0, 0)),
            pl.BlockSpec(memory_space=pl.ANY),
            pl.BlockSpec((NATOM, batches), lambda p, i: (0, 0)),
        ],
        out_specs=(
            pl.BlockSpec((batches, points // SIDE), lambda p, i: (0, 0)),
            pl.BlockSpec((components, NATOM), lambda p, i: (0, 0)),
        ),
        out_shape=(
            jax.ShapeDtypeStruct((batches, points // SIDE), jnp.float32),
            jax.ShapeDtypeStruct((components, NATOM), jnp.float32),
        ),
        scratch_shapes=[
            pltpu.VMEM((PASSES, rows, LANES), jnp.bfloat16),
            pltpu.VMEM((PASSES * 2 * BLOCK, LANES), jnp.float32),
            pltpu.VMEM((PASSES, BLOCK, LANES), jnp.bfloat16),
            pltpu.VMEM((rows + 8, LANES), jnp.float32),
            pltpu.VMEM((slots * GROUPS, LANES), jnp.float32),
            pltpu.VMEM((slots * GROUPS, LANES), jnp.float32),
            pltpu.VMEM((UNROLL, points, LANES), jnp.float32),
            pltpu.VMEM((components, batches, points), jnp.float32),
            pltpu.VMEM((SIDE, batches, LANES), jnp.float32),
            pltpu.VMEM((SIDE, batches, LANES), jnp.float32),
            pltpu.VMEM((2 * SIDE, NATOM, LANES), jnp.float32),
            pltpu.VMEM((SIDE, NATOM, LANES), jnp.float32),
            pltpu.VMEM((SIDE, NATOM, LANES), jnp.float32),
            pltpu.SemaphoreType.DMA((PASSES * 2 * MESSAGES + PASSES,)),
            pltpu.SemaphoreType.DMA((PASSES * 2 * MESSAGES + PASSES,)),
            pltpu.SemaphoreType.DMA((16,)),
            pltpu.SemaphoreType.DMA((16,)),
            pltpu.SemaphoreType.DMA,
        ],
        compiler_params=pltpu.CompilerParams(
            collective_id=0, has_side_effects=True, vmem_limit_bytes=48 * 2**20,
            dimension_semantics=("arbitrary", "arbitrary"),
        ),
    )(
        idx, coeffs, occupation.reshape(PASSES, GROUPS, LANES), basis_on_grid,
        harmonics.transpose(1, 0, 2), member,
    )
    return density, moments.T


def solution(mesh):
    placed = (
        P("row", "col"),
        P("col"),
        P("row", None, None),
        P("row", None),
        P("row"),
        P("row"),
        P("row", None, None),
    )
    return jax.shard_map(shards, mesh=mesh, in_specs=placed, out_specs=(P("row", "col"), P()), check_vma=False)
```

time: 259 us -> 115 us (0.44)
  Pallas kernels: 0 us -> 106 us
  local copies, waits for them, and re-layouts: 109 us -> 5.06 us
  waiting for transfers between devices: 76 us -> 0 us
  matrix products: 36.7 us -> 0 us
  between operations: 14.1 us -> 0.67 us
  blocking collectives: 12 us -> 0 us
  starting transfers between devices: 5.46 us -> 0 us
    pallas_call x0 -> x1, Pallas kernels: none -> 106 us  [shards(): pl.pallas_call(kernel, grid=(PASSES, batches // UNROLL), in_specs=[pl.Blo...]
    gather x1 -> x0, local copies, waits for them, and re-layouts: 106 us -> none  [shards(): selected = jnp.take(whole, basis_map, axis=0)]
    all_gather x1 -> x0, waiting for transfers between devices: 65.6 us -> none  [shards(): whole = lax.all_gather(coeffs, 'row', axis=0, tiled=True)]
    dot_general x3 -> x0, matrix products: 36.7 us -> none  [the longest x1 28.6 us: shards(): jnp.einsum('bps,bsk->bpk', masked, selected, preferred_element_type=jnp.f...]
    all_to_all x1 -> x0, blocking collectives: 12 us -> none  [sent_to_all(): return lax.all_to_all(copies, axis, split_axis=0, concat_axis=0, tiled=True)]
    all_to_all x1 -> x0, waiting for transfers between devices: 9.74 us -> none  [sent_to_all(): return lax.all_to_all(copies, axis, split_axis=0, concat_axis=0, tiled=True)]
    all_to_all x1 -> x0, starting transfers between devices: 5.42 us -> none  [sent_to_all(): return lax.all_to_all(copies, axis, split_axis=0, concat_axis=0, tiled=True)]
    unnamed x8 -> x9, local copies, waits for them, and re-layouts: 1.55 us -> 5.06 us
  transfers between devices with their start and end apart: 2 -> 0, of which waited for: 2 -> 0; matrix products, arithmetic and copies ran while one was open for 1% -> 0% of each run, Pallas kernels for 0% -> 0%
where the time goes in v3:
time: 115 us
  Pallas kernels  106 us (92%)
  local copies, waits for them, and re-layouts  5.06 us (4%)
  other arithmetic  2.66 us (2%)
    pallas_call x1, Pallas kernels, shards(): pl.pallas_call(kernel, grid=(PASSES, batches // UNROLL), in_specs=[pl.Blo...  106 us
    unnamed x9, local copies, waits for them, and re-layouts  5.06 us

profile of v3, /device:TPU:0, one launch (start us, length us, event | category | flops | bytes accessed | tf_op | source)
XLA Modules:
  0.0 114.8 jit_solution(18030474542166360628)
XLA Ops:
  0.6 1.0 fusion.7
  1.7 1.0 fusion.4
  2.7 0.7 fusion.6.member_ref
  3.3 0.0 copy-start
  3.3 2.1 %copy-done = f32[40,49,512]{2,0,1:T(8,128)S(1)} copy-done((f32[40,49,512]{2,0,1:T(8,128)S(1)}, f32[40,49,512]{2,0,1:T(8,128)}, u32[]{:S(2)}) %copy-start) | copy-done | bytes 4014104
  5.5 0.0 copy-start.1
  5.5 1.0 copy-done.1
  6.5 0.0 copy-start.2
  6.5 0.7 copy-done.2
  7.2 106.4 %shard_map.86 = (f32[40,128]{1,0:T(8,128)S(1)}, f32[49,64]{1,0:T(8,128)S(1)}) custom-call(s32[20992]{0:T(1024)S(1)} %pad_add_fusion.idx_ref, bf16[192,1024]{1,0:T(8,128)(2,1)S(1)} %copy-done.1, f32[2,4,128]{2,1,0:T(4,128)S(1)} %bitcast.9, bf16[40,512,512]{2,1,0:T(8,128)(2,1)} %m_ref.1, f32[49,40,512]{2,1,0:T(8,128)S(1)} %bitcast.7, ...), custom_call_target="tpu_custom_call" | custom-call | tf_op jit(solution)/shard_map/pallas_call | solution.py:295
  113.6 0.6 copy.12
  114.2 0.6 copy.13
  (3 shorter events, 0.0 us)
Async XLA Ops:
  3.3 2.1 %copy-start = (f32[40,49,512]{2,0,1:T(8,128)S(1)}, f32[40,49,512]{2,0,1:T(8,128)}, u32[]{:S(2)}) copy-start(f32[40,49,512]{2,0,1:T(8,128)} %param.13) | copy-start | bytes 12042244
  5.5 1.0 copy-start.1
  6.5 0.7 copy-start.2

commit v4 on v3

v4 whole, which is shorter than its diff:
```python
import jax
import jax.numpy as jnp
from jax import lax
from jax.experimental import pallas as pl
from jax.experimental.pallas import tpu as pltpu
from jax.sharding import PartitionSpec as P

NATOM = 64
WIN = 96
LANES = 128
SIDE = 4
GROUPS = 8
PAD = GROUPS + 1
BLOCK = WIN * GROUPS
UNROLL = 4
MESH = pl.DeviceIdType.MESH
OFFSETS = ((0, 0), (-1, 0), (1, 0), (2, 0))
MESSAGES = 20


def message(number):
    if number < 2:
        return (0, 0), (1 - 2 * number, 0), None
    if number < 4:
        return (2 * number - 5, 0), (5 - 2 * number, 0), number - 2
    k, down = (number - 4) // 2 % 4, number % 2
    if number < 12:
        return OFFSETS[k], (0, 1 - 2 * down), None
    return (OFFSETS[k][0], 2 * down - 1), (0, 1 - 2 * down), down


def arrival(number):
    at, to, half = message(number)
    first, second = at[0] - to[0], at[1] - to[1]
    return (2 if first == -2 else first, 2 if second == -2 else second), half


def kernel(
    idx_ref, coeffs_ref, occ_ref, m_ref, harm_hbm, member_ref, density_ref, moments_ref,
    window, staged, other, wide, even, odd, acc, harm, part, parts, column, line, plane,
    send_sem, recv_sem, sum_send, sum_recv, harm_sem,
):
    step, steps = pl.program_id(0), pl.num_programs(0)
    me = lax.axis_index("row")
    z = lax.axis_index("col")
    y, x, core = me // (2 * SIDE), (me // 2) % SIDE, me % 2
    slots = m_ref.shape[2]
    rows = window.shape[0]

    def row_of(dy, dx):
        return (lax.rem(y + dy + SIDE, SIDE) * SIDE + lax.rem(x + dx + SIDE, SIDE)) * 2 + core

    def turned(first, second, turn):
        return first * turn + second * (1 - turn), first * (1 - turn) + second * turn

    def rows_at(at, turn, half):
        q = row_of(*turned(*at, turn)) - core + turn
        if half is None:
            return pl.ds(pl.multiple_of(q * BLOCK, BLOCK), BLOCK)
        return pl.ds(pl.multiple_of(q * BLOCK + half * (BLOCK // 2), BLOCK // 2), BLOCK // 2)

    def copy(turn, number, at, half):
        to = message(number)[1]
        place = window.at[rows_at(at, turn, half)]
        sem = turn * MESSAGES + number
        return pltpu.make_async_remote_copy(
            src_ref=place, dst_ref=place, send_sem=send_sem.at[sem], recv_sem=recv_sem.at[sem],
            device_id=(row_of(*turned(*to, turn)), z), device_id_type=MESH,
        )

    def outgoing(turn, number):
        at, _, half = message(number)
        return copy(turn, number, at, half)

    def send(turn, *numbers):
        for number in numbers:
            outgoing(turn, number).start()

    def arrive(turn, *numbers):
        for number in numbers:
            at, half = arrival(number)
            copy(turn, number, at, half).wait_recv()

    a, b = core, 1 - core
    partner = me - core + b

    def swap(turn):
        return pltpu.make_async_remote_copy(
            src_ref=other, dst_ref=window.at[rows_at((0, 0), turn, None)],
            send_sem=send_sem.at[2 * MESSAGES], recv_sem=recv_sem.at[2 * MESSAGES],
            device_id=(partner, z), device_id_type=MESH,
        )

    def outward(turn):
        send(turn, 0, 1, 4, 5)

    def first_hop(turn):
        arrive(turn, 0)
        send(turn, 2)
        arrive(turn, 1)
        send(turn, 3, 6, 7, 8, 9)

    def second_hop(turn):
        arrive(turn, 2, 3)
        send(turn, 10, 11)

    def onward(turn, k):
        arrive(turn, 4 + 2 * k)
        send(turn, 12 + 2 * k)
        arrive(turn, 5 + 2 * k)
        send(turn, 13 + 2 * k)

    def widen(turn, at):
        held = rows_at(at, turn, None)
        wide[held, :] = window[held, :].astype(jnp.float32)

    pairs = [(dz, dc) for dz in range(SIDE) for dc in range(2) if (dz, dc) != (0, 0)]

    def column_device(dz, dc):
        return me - core + lax.rem(core + dc, 2), lax.rem(z + dz, SIDE)

    def pick(into, batch, low, high):
        for s in range(low, high):
            into[pl.ds(s * PAD, GROUPS), :] = wide[pl.ds(idx_ref[batch * slots + s], GROUPS), :]

    harm_copy = pltpu.make_async_copy(harm_hbm, harm, harm_sem)

    @pl.when(step == 0)
    def _():
        harm_copy.start()
        for j in range(GROUPS):
            staged[pl.ds(j, 2 * WIN, stride=GROUPS), :] = coeffs_ref[:, j * LANES : (j + 1) * LANES].astype(
                jnp.float32
            )
        other[...] = staged[pl.ds(pl.multiple_of(b * BLOCK, BLOCK), BLOCK), :].astype(jnp.bfloat16)
        window[rows_at((0, 0), a, None), :] = staged[pl.ds(pl.multiple_of(a * BLOCK, BLOCK), BLOCK), :].astype(
            jnp.bfloat16
        )
        barrier = pltpu.get_barrier_semaphore()
        near = [column_device(*p) for p in pairs]
        near += [(row_of(0, d), z) for d in (1, 2, 3)] + [(row_of(d, 0), z) for d in (1, 2, 3)]
        for device in near:
            pl.semaphore_signal(barrier, inc=1, device_id=device, device_id_type=MESH)
        pl.semaphore_wait(barrier, len(near))
        swap(a).start()
        outward(a)
        swap(b).wait_recv()
        outward(b)
        wide[pl.ds(rows, 8), :] = jnp.zeros((8, LANES), jnp.float32)
        for turn in (a, b):
            first_hop(turn)
            onward(turn, 0)
        for turn in (a, b):
            second_hop(turn)
        for k in (1, 2, 3):
            for turn in (a, b):
                onward(turn, k)
        for turn in (a, b):
            for first, _ in OFFSETS:
                for second in (0, -1, 1):
                    widen(turn, (first, second))
        for k in range(4):
            for turn in (a, b):
                arrive(turn, 12 + 2 * k, 13 + 2 * k)
                widen(turn, (OFFSETS[k][0], 2))
        pick(even, 0, 0, slots)

    for which in range(UNROLL):
        held, into = (even, odd) if which % 2 == 0 else (odd, even)
        batch = UNROLL * step + which
        tiles = GROUPS // 2
        for tile in range(tiles):
            pick(into, batch + 1, tile * slots // tiles, (tile + 1) * slots // tiles)
            groups = (2 * tile, 2 * tile + 1)
            right = jnp.concatenate(
                [held[pl.ds(j, slots, stride=PAD), :].astype(jnp.bfloat16) for j in groups], axis=1
            )
            orbital = jnp.dot(m_ref[which], right, preferred_element_type=jnp.float32)
            first, second = orbital[:, :LANES], orbital[:, LANES:]
            term = first * first * occ_ref[groups[0] : groups[0] + 1, :]
            term += second * second * occ_ref[groups[1] : groups[1] + 1, :]
            acc[which] = term if tile == 0 else acc[which] + term
        row = jnp.sum(acc[which].T, axis=0, keepdims=True)
        for c in range(SIDE):
            part[c, pl.ds(batch, 1), :] = row[:, c * LANES : (c + 1) * LANES]

    @pl.when(step == steps - 1)
    def _():
        def remote(ref, slot, source, number, device):
            return pltpu.make_async_remote_copy(
                src_ref=source, dst_ref=ref.at[slot], send_sem=sum_send.at[number], recv_sem=sum_recv.at[number],
                device_id=device, device_id_type=MESH,
            )

        densities = [
            remote(parts, z, part.at[lax.rem(z + dz, SIDE)], 6 + dz, column_device(dz, 0)) for dz in (1, 2, 3)
        ]
        for one in densities:
            one.start()
        parts[z] = part[z]
        harm_copy.wait()
        lane = lax.broadcasted_iota(jnp.int32, (part.shape[1], LANES), 1)
        local = jnp.zeros((part.shape[1], LANES), jnp.float32)
        for l in range(harm.shape[0]):
            product = harm[l, :, :LANES] * part[0]
            for c in range(1, SIDE):
                product += harm[l, :, c * LANES : (c + 1) * LANES] * part[c]
            local = jnp.where(lane % NATOM == l, jnp.sum(product, axis=1, keepdims=True), local)
        slot = z * 2 + core
        by_atom = jnp.dot(
            member_ref[...], local, precision=lax.Precision.HIGHEST, preferred_element_type=jnp.float32
        )
        low = lax.broadcasted_iota(jnp.int32, (NATOM // 2, LANES), 1) < NATOM
        column[slot] = jnp.where(low, by_atom[: NATOM // 2], by_atom[NATOM // 2 :])
        columns = [remote(column, slot, column.at[slot], n, column_device(*p)) for n, p in enumerate(pairs)]
        for one in columns:
            one.start()
        for dz in (1, 2, 3):
            source = lax.rem(z - dz + SIDE, SIDE)
            remote(parts, source, part.at[0], 6 + dz, column_device(dz, 0)).wait_recv()
        density_ref[...] = parts[0] + parts[1] + parts[2] + parts[3]
        for n, (dz, dc) in enumerate(pairs):
            source = lax.rem(z - dz + SIDE, SIDE) * 2 + lax.rem(core + dc, 2)
            remote(column, source, column.at[source], n, column_device(dz, dc)).wait_recv()
        here = column[0]
        for s in range(1, 2 * SIDE):
            here = here + column[s]
        line[x] = here
        lines = [remote(line, x, line.at[x], 9 + d, (row_of(0, d), z)) for d in (1, 2, 3)]
        for one in lines:
            one.start()
        for d in (1, 2, 3):
            source = lax.rem(x - d + SIDE, SIDE)
            remote(line, source, line.at[source], 9 + d, (row_of(0, d), z)).wait_recv()
        plane[y] = line[0] + line[1] + line[2] + line[3]
        planes = [remote(plane, y, plane.at[y], 12 + d, (row_of(d, 0), z)) for d in (1, 2, 3)]
        for one in planes:
            one.start()
        for d in (1, 2, 3):
            source = lax.rem(y - d + SIDE, SIDE)
            remote(plane, source, plane.at[source], 12 + d, (row_of(d, 0), z)).wait_recv()
        turned_over = (plane[0] + plane[1] + plane[2] + plane[3]).T
        components = moments_ref.shape[0]
        moments_ref[:, : NATOM // 2] = turned_over[:components, :]
        moments_ref[:, NATOM // 2 :] = turned_over[NATOM : NATOM + components, :]
        for one in densities + columns + lines + planes:
            one.wait_send()
        swap(a).wait_send()
        for turn in (a, b):
            for number in range(MESSAGES):
                outgoing(turn, number).wait_send()


def shards(coeffs, occupation, basis_on_grid, basis_map, basis_count, batch_atom, harmonics):
    batches, points, slots = basis_on_grid.shape
    components = harmonics.shape[1]
    parity = lax.rem(lax.axis_index("row"), 2)
    shard = coeffs.shape[0]
    rows = 2 * SIDE * SIDE * BLOCK
    place = (basis_map // shard) * WIN + basis_map % shard - parity * WIN
    slot_ids = lax.broadcasted_iota(jnp.int32, (batches, slots), 1)
    place = jnp.where(slot_ids < basis_count[:, None], place * GROUPS, rows)
    idx = jnp.concatenate([place.reshape(-1), place[0]])
    member = (lax.broadcasted_iota(jnp.int32, (NATOM, batches), 0) == batch_atom[None, :]).astype(jnp.float32)
    density, moments = pl.pallas_call(
        kernel,
        grid=(batches // UNROLL,),
        in_specs=[
            pl.BlockSpec(memory_space=pltpu.SMEM),
            pl.BlockSpec(coeffs.shape, lambda i: (0, 0)),
            pl.BlockSpec((GROUPS, LANES), lambda i: (0, 0)),
            pl.BlockSpec((UNROLL, points, slots), lambda i: (i, 0, 0)),
            pl.BlockSpec(memory_space=pl.ANY),
            pl.BlockSpec((NATOM, batches), lambda i: (0, 0)),
        ],
        out_specs=(
            pl.BlockSpec((batches, points // SIDE), lambda i: (0, 0)),
            pl.BlockSpec((components, NATOM), lambda i: (0, 0)),
        ),
        out_shape=(
            jax.ShapeDtypeStruct((batches, points // SIDE), jnp.float32),
            jax.ShapeDtypeStruct((components, NATOM), jnp.float32),
        ),
        scratch_shapes=[
            pltpu.VMEM((rows, LANES), jnp.bfloat16),
            pltpu.VMEM((2 * BLOCK, LANES), jnp.float32),
            pltpu.VMEM((BLOCK, LANES), jnp.bfloat16),
            pltpu.VMEM((rows + 8, LANES), jnp.float32),
            pltpu.VMEM((slots * PAD + 8, LANES), jnp.float32),
            pltpu.VMEM((slots * PAD + 8, LANES), jnp.float32),
            pltpu.VMEM((UNROLL, points, LANES), jnp.float32),
            pltpu.VMEM((components, batches, points), jnp.float32),
            pltpu.VMEM((SIDE, batches, LANES), jnp.float32),
            pltpu.VMEM((SIDE, batches, LANES), jnp.float32),
            pltpu.VMEM((2 * SIDE, NATOM // 2, LANES), jnp.float32),
            pltpu.VMEM((SIDE, NATOM // 2, LANES), jnp.float32),
            pltpu.VMEM((SIDE, NATOM // 2, LANES), jnp.float32),
            pltpu.SemaphoreType.DMA((2 * MESSAGES + 1,)),
            pltpu.SemaphoreType.DMA((2 * MESSAGES + 1,)),
            pltpu.SemaphoreType.DMA((16,)),
            pltpu.SemaphoreType.DMA((16,)),
            pltpu.SemaphoreType.DMA,
        ],
        compiler_params=pltpu.CompilerParams(
            collective_id=0, has_side_effects=True, vmem_limit_bytes=60 * 2**20,
            dimension_semantics=("arbitrary",),
        ),
    )(
        idx, coeffs, occupation.reshape(GROUPS, LANES), basis_on_grid,
        harmonics.transpose(1, 0, 2), member,
    )
    return density, moments.T


def solution(mesh):
    placed = (
        P("row", "col"),
        P("col"),
        P("row", None, None),
        P("row", None),
        P("row"),
        P("row"),
        P("row", None, None),
    )
    return jax.shard_map(shards, mesh=mesh, in_specs=placed, out_specs=(P("row", "col"), P()), check_vma=False)
```

time: 115 us -> 97.3 us (0.85)
  Pallas kernels: 106 us -> 89.7 us
  local copies, waits for them, and re-layouts: 5.06 us -> 2.72 us
  other arithmetic: 2.66 us -> 3.9 us
    pallas_call x1, Pallas kernels: 106 us -> 89.7 us  [shards(): pl.pallas_call(kernel, grid=(batches // UNROLL,), in_specs=[pl.BlockSpec(...]
    unnamed x9 -> x3, local copies, waits for them, and re-layouts: 5.06 us -> 2.72 us
where the time goes in v4:
time: 97.3 us; the launch traced here: 97 us
  Pallas kernels  89.7 us (92%)
  other arithmetic  3.9 us (4%)
  local copies, waits for them, and re-layouts  2.72 us (3%)
    pallas_call x1, Pallas kernels, shards(): pl.pallas_call(kernel, grid=(batches // UNROLL,), in_specs=[pl.BlockSpec(...  89.7 us
    unnamed x3, local copies, waits for them, and re-layouts  2.72 us

profile of v4, /device:TPU:0, one launch (start us, length us, event | category | flops | bytes accessed | tf_op | source)
XLA Modules:
  0.0 97.0 jit_solution(4201453687520193493)
XLA Ops:
  0.6 1.0 %fusion.7 = s32[5,4,8,128]{3,2,1,0:T(8,128)S(1)} fusion(s32[]{:T(128)S(6)} %mul.17, s32[40,512]{1,0:T(8,128)} %param.10, s32[40]{0:T(128)} %param.11), kind=kLoop, calls=%fused_computation.14 | loop fusion | flops 368640 | bytes 164004
  1.7 1.0 %fusion.4 = s32[40,512]{1,0:T(8,128)S(1)} fusion(s32[40,512]{1,0:T(8,128)} %param.10, s32[]{:T(128)S(6)} %mul.17, s32[40]{0:T(128)} %param.11), kind=kLoop, calls=%fused_computation.7 | loop fusion | flops 368640 | bytes 164004 | tf_op jit(solution)/shard_map/jit(_where)/select_n | solution.py:262
  2.7 0.6 pad_add_fusion.idx_ref
  3.3 1.3 %fusion.6.member_ref = f32[64,40]{1,0:T(8,128)} fusion(s32[40]{0:T(128)} %param.12), kind=kLoop, calls=%fused_computation.13 | loop fusion | flops 5120 | bytes 10400 | tf_op jit(solution)/shard_map/convert_element_type | solution.py:264
  4.6 89.7 %shard_map.86 = (f32[40,128]{1,0:T(8,128)}, f32[49,64]{1,0:T(8,128)}) custom-call(s32[20992]{0:T(1024)} %pad_add_fusion.idx_ref, bf16[192,1024]{1,0:T(8,128)(2,1)} %coeffs_ref.1, f32[8,128]{1,0:T(8,128)} %bitcast.11, bf16[40,512,512]{2,1,0:T(8,128)(2,1)} %m_ref.1, f32[49,40,512]{2,1,0:T(8,128)} %bitcast.7, f32[64,40]{1,0:T(8,128)} %fusion.6.member_ref), custom_call_target="tpu_custom_call" | custom-call | tf_op jit(solution)/shard_map/pallas_call | solution.py:265
  94.3 1.3 %copy.12 = f32[40,128]{1,0:T(8,128)} copy(f32[40,128]{1,0:T(8,128)} %get-tuple-element.8) | data formatting | bytes 40960
  95.6 1.4 %copy.13 = f32[64,49]{0,1:T(8,128)} copy(f32[64,49]{0,1:T(8,128)} %bitcast.9) | data formatting | bytes 25088
  (2 shorter events, 0.0 us)

commit v5 on v4

--- a/solution.py
+++ b/solution.py
@@ -36,15 +36,15 @@
 
 
 def kernel(
-    idx_ref, coeffs_ref, occ_ref, m_ref, harm_hbm, member_ref, density_ref, moments_ref,
-    window, staged, other, wide, even, odd, acc, harm, part, parts, column, line, plane,
-    send_sem, recv_sem, sum_send, sum_recv, harm_sem,
+    idx_ref, coeffs_ref, occ_ref, m_hbm, harm_hbm, member_ref, density_ref, moments_ref,
+    window, staged, other, wide, even, odd, acc, values, harm, part, parts, column, line, plane,
+    send_sem, recv_sem, sum_send, sum_recv, values_sem, harm_sem,
 ):
     step, steps = pl.program_id(0), pl.num_programs(0)
     me = lax.axis_index("row")
     z = lax.axis_index("col")
     y, x, core = me // (2 * SIDE), (me // 2) % SIDE, me % 2
-    slots = m_ref.shape[2]
+    batches, _, slots = m_hbm.shape
     rows = window.shape[0]
 
     def row_of(dy, dx):
@@ -123,11 +123,20 @@
         for s in range(low, high):
             into[pl.ds(s * PAD, GROUPS), :] = wide[pl.ds(idx_ref[batch * slots + s], GROUPS), :]
 
+    def values_copy(at, slot):
+        batch = pl.multiple_of(at * UNROLL, UNROLL)
+        return pltpu.make_async_copy(m_hbm.at[pl.ds(batch, UNROLL)], values.at[slot], values_sem.at[slot])
+
     harm_copy = pltpu.make_async_copy(harm_hbm, harm, harm_sem)
 
     @pl.when(step == 0)
     def _():
-        harm_copy.start()
+        barrier = pltpu.get_barrier_semaphore()
+        near = [column_device(*p) for p in pairs]
+        near += [(row_of(0, d), z) for d in (1, 2, 3)] + [(row_of(d, 0), z) for d in (1, 2, 3)]
+        for device in near:
+            pl.semaphore_signal(barrier, inc=1, device_id=device, device_id_type=MESH)
+        values_copy(0, 0).start()
         for j in range(GROUPS):
             staged[pl.ds(j, 2 * WIN, stride=GROUPS), :] = coeffs_ref[:, j * LANES : (j + 1) * LANES].astype(
                 jnp.float32
@@ -136,17 +145,13 @@
         window[rows_at((0, 0), a, None), :] = staged[pl.ds(pl.multiple_of(a * BLOCK, BLOCK), BLOCK), :].astype(
             jnp.bfloat16
         )
-        barrier = pltpu.get_barrier_semaphore()
-        near = [column_device(*p) for p in pairs]
-        near += [(row_of(0, d), z) for d in (1, 2, 3)] + [(row_of(d, 0), z) for d in (1, 2, 3)]
-        for device in near:
-            pl.semaphore_signal(barrier, inc=1, device_id=device, device_id_type=MESH)
+        wide[pl.ds(rows, 8), :] = jnp.zeros((8, LANES), jnp.float32)
         pl.semaphore_wait(barrier, len(near))
         swap(a).start()
         outward(a)
         swap(b).wait_recv()
         outward(b)
-        wide[pl.ds(rows, 8), :] = jnp.zeros((8, LANES), jnp.float32)
+        harm_copy.start()
         for turn in (a, b):
             first_hop(turn)
             onward(turn, 0)
@@ -165,17 +170,25 @@
                 widen(turn, (OFFSETS[k][0], 2))
         pick(even, 0, 0, slots)
 
+    turn_of = lax.rem(step, 2)
+    values_copy(step, turn_of).wait()
+
+    @pl.when(step + 1 < steps)
+    def _():
+        values_copy(step + 1, 1 - turn_of).start()
+
     for which in range(UNROLL):
         held, into = (even, odd) if which % 2 == 0 else (odd, even)
         batch = UNROLL * step + which
+        after = jnp.minimum(batch + 1, batches - 1)
         tiles = GROUPS // 2
         for tile in range(tiles):
-            pick(into, batch + 1, tile * slots // tiles, (tile + 1) * slots // tiles)
+            pick(into, after, tile * slots // tiles, (tile + 1) * slots // tiles)
             groups = (2 * tile, 2 * tile + 1)
             right = jnp.concatenate(
                 [held[pl.ds(j, slots, stride=PAD), :].astype(jnp.bfloat16) for j in groups], axis=1
             )
-            orbital = jnp.dot(m_ref[which], right, preferred_element_type=jnp.float32)
+            orbital = jnp.dot(values[turn_of, which], right, preferred_element_type=jnp.float32)
             first, second = orbital[:, :LANES], orbital[:, LANES:]
             term = first * first * occ_ref[groups[0] : groups[0] + 1, :]
             term += second * second * occ_ref[groups[1] : groups[1] + 1, :]
@@ -260,7 +273,7 @@
     place = (basis_map // shard) * WIN + basis_map % shard - parity * WIN
     slot_ids = lax.broadcasted_iota(jnp.int32, (batches, slots), 1)
     place = jnp.where(slot_ids < basis_count[:, None], place * GROUPS, rows)
-    idx = jnp.concatenate([place.reshape(-1), place[0]])
+    idx = place.reshape(-1)
     member = (lax.broadcasted_iota(jnp.int32, (NATOM, batches), 0) == batch_atom[None, :]).astype(jnp.float32)
     density, moments = pl.pallas_call(
         kernel,
@@ -269,8 +282,8 @@
             pl.BlockSpec(memory_space=pltpu.SMEM),
             pl.BlockSpec(coeffs.shape, lambda i: (0, 0)),
             pl.BlockSpec((GROUPS, LANES), lambda i: (0, 0)),
-            pl.BlockSpec((UNROLL, points, slots), lambda i: (i, 0, 0)),
-            pl.BlockSpec(memory_space=pl.ANY),
+            pl.BlockSpec(memory_space=pltpu.HBM),
+            pl.BlockSpec(memory_space=pltpu.HBM),
             pl.BlockSpec((NATOM, batches), lambda i: (0, 0)),
         ],
         out_specs=(
@@ -289,6 +302,7 @@
             pltpu.VMEM((slots * PAD + 8, LANES), jnp.float32),
             pltpu.VMEM((slots * PAD + 8, LANES), jnp.float32),
             pltpu.VMEM((UNROLL, points, LANES), jnp.float32),
+            pltpu.VMEM((2, UNROLL, points, slots), jnp.bfloat16),
             pltpu.VMEM((components, batches, points), jnp.float32),
             pltpu.VMEM((SIDE, batches, LANES), jnp.float32),
             pltpu.VMEM((SIDE, batches, LANES), jnp.float32),
@@ -299,10 +313,11 @@
             pltpu.SemaphoreType.DMA((2 * MESSAGES + 1,)),
             pltpu.SemaphoreType.DMA((16,)),
             pltpu.SemaphoreType.DMA((16,)),
+            pltpu.SemaphoreType.DMA((2,)),
             pltpu.SemaphoreType.DMA,
         ],
         compiler_params=pltpu.CompilerParams(
-            collective_id=0, has_side_effects=True, vmem_limit_bytes=60 * 2**20,
+            collective_id=0, has_side_effects=True, vmem_limit_bytes=52 * 2**20,
             dimension_semantics=("arbitrary",),
         ),
     )(

time: 97.3 us -> 95.7 us (0.984)
  other arithmetic: 3.9 us -> 1.66 us
    select_n x1 -> x0, other arithmetic: 1 us -> none  [shards(): place = jnp.where(slot_ids < basis_count[:, None], place * GROUPS, rows)]
    unnamed x3 -> x7, local copies, waits for them, and re-layouts: 2.72 us -> 2.92 us
where the time goes in v5:
time: 95.7 us; the launch traced here: 95.5 us
  Pallas kernels  90.3 us (94%)
  local copies, waits for them, and re-layouts  2.92 us (3%)
  other arithmetic  1.66 us (2%)
    pallas_call x1, Pallas kernels, shards(): pl.pallas_call(kernel, grid=(batches // UNROLL,), in_specs=[pl.BlockSpec(...  90.3 us
    unnamed x7, local copies, waits for them, and re-layouts  2.92 us

profile of v5, /device:TPU:0, one launch (start us, length us, event | category | flops | bytes accessed | tf_op | source)
XLA Modules:
  0.0 95.5 jit_solution(15704565423167367920)
XLA Ops:
  0.6 1.0 %fusion.5 = s32[5,4,8,128]{3,2,1,0:T(8,128)S(1)} fusion(s32[40,512]{1,0:T(8,128)} %param.10, s32[]{:T(128)S(6)} %mul.17, s32[40]{0:T(128)} %param.11), kind=kLoop, calls=%fused_computation.7 | loop fusion | flops 368640 | bytes 164004
  1.7 0.7 fusion.7.member_ref
  2.3 0.0 copy-start
  2.3 1.0 %copy-done = bf16[192,1024]{1,0:T(8,128)(2,1)S(1)} copy-done((bf16[192,1024]{1,0:T(8,128)(2,1)S(1)}, bf16[192,1024]{1,0:T(8,128)(2,1)}, u32[]{:S(2)}) %copy-start) | copy-done | bytes 393240
  3.3 0.0 copy-start.1
  3.3 0.7 copy-done.1
  4.0 90.3 %shard_map.86 = (f32[40,128]{1,0:T(8,128)S(1)}, f32[49,64]{1,0:T(8,128)S(1)}) custom-call(s32[20480]{0:T(1024)S(1)} %bitcast.6, bf16[192,1024]{1,0:T(8,128)(2,1)S(1)} %copy-done, f32[8,128]{1,0:T(8,128)S(1)} %bitcast.8, bf16[40,512,512]{2,1,0:T(8,128)(2,1)} %m_hbm.1, f32[49,40,512]{2,1,0:T(8,128)} %bitcast.9, f32[64,40]{1,0:T(8,128)S(1)} %fusion.7.member_ref), custom_call_target="tpu_custom_call" | custom-call | tf_op jit(solution)/shard_map/pallas_call | solution.py:278
  94.3 0.6 copy.12
  94.9 0.6 copy.13
  (1 shorter events, 0.0 us)
Async XLA Ops:
  2.3 1.0 %copy-start = (bf16[192,1024]{1,0:T(8,128)(2,1)S(1)}, bf16[192,1024]{1,0:T(8,128)(2,1)}, u32[]{:S(2)}) copy-start(bf16[192,1024]{1,0:T(8,128)(2,1)} %coeffs_ref.1) | copy-start | bytes 1179652
  3.3 0.7 copy-start.1

commit v6 on v5

--- a/solution.py
+++ b/solution.py
@@ -10,6 +10,7 @@
 LANES = 128
 SIDE = 4
 GROUPS = 8
+TILE = 4
 PAD = GROUPS + 1
 BLOCK = WIN * GROUPS
 UNROLL = 4
@@ -171,6 +172,8 @@
         pick(even, 0, 0, slots)
 
     turn_of = lax.rem(step, 2)
+    none = jnp.minimum(step, 0)
+    spare, zeros = pl.ds(slots * PAD + none, 8), pl.ds(rows + none, 8)
     values_copy(step, turn_of).wait()
 
     @pl.when(step + 1 < steps)
@@ -181,18 +184,23 @@
         held, into = (even, odd) if which % 2 == 0 else (odd, even)
         batch = UNROLL * step + which
         after = jnp.minimum(batch + 1, batches - 1)
-        tiles = GROUPS // 2
+        tiles = GROUPS // TILE
         for tile in range(tiles):
             pick(into, after, tile * slots // tiles, (tile + 1) * slots // tiles)
-            groups = (2 * tile, 2 * tile + 1)
+            groups = range(TILE * tile, TILE * (tile + 1))
             right = jnp.concatenate(
                 [held[pl.ds(j, slots, stride=PAD), :].astype(jnp.bfloat16) for j in groups], axis=1
             )
             orbital = jnp.dot(values[turn_of, which], right, preferred_element_type=jnp.float32)
-            first, second = orbital[:, :LANES], orbital[:, LANES:]
-            term = first * first * occ_ref[groups[0] : groups[0] + 1, :]
-            term += second * second * occ_ref[groups[1] : groups[1] + 1, :]
+            term = None
+            for n, j in enumerate(groups):
+                one = orbital[:, n * LANES : (n + 1) * LANES]
+                square = one * one * occ_ref[j : j + 1, :]
+                term = square if term is None else term + square
             acc[which] = term if tile == 0 else acc[which] + term
+            held[spare, :] = jnp.zeros((8, LANES), jnp.float32)
+            wide[zeros, :] = held[spare, :]
+            held[spare, :] = wide[zeros, :]
         row = jnp.sum(acc[which].T, axis=0, keepdims=True)
         for c in range(SIDE):
             part[c, pl.ds(batch, 1), :] = row[:, c * LANES : (c + 1) * LANES]
@@ -208,9 +216,6 @@
         densities = [
             remote(parts, z, part.at[lax.rem(z + dz, SIDE)], 6 + dz, column_device(dz, 0)) for dz in (1, 2, 3)
         ]
-        for one in densities:
-            one.start()
-        parts[z] = part[z]
         harm_copy.wait()
         lane = lax.broadcasted_iota(jnp.int32, (part.shape[1], LANES), 1)
         local = jnp.zeros((part.shape[1], LANES), jnp.float32)
@@ -228,10 +233,9 @@
         columns = [remote(column, slot, column.at[slot], n, column_device(*p)) for n, p in enumerate(pairs)]
         for one in columns:
             one.start()
-        for dz in (1, 2, 3):
-            source = lax.rem(z - dz + SIDE, SIDE)
-            remote(parts, source, part.at[0], 6 + dz, column_device(dz, 0)).wait_recv()
-        density_ref[...] = parts[0] + parts[1] + parts[2] + parts[3]
+        for one in densities:
+            one.start()
+        parts[z] = part[z]
         for n, (dz, dc) in enumerate(pairs):
             source = lax.rem(z - dz + SIDE, SIDE) * 2 + lax.rem(core + dc, 2)
             remote(column, source, column.at[source], n, column_device(dz, dc)).wait_recv()
@@ -242,6 +246,10 @@
         lines = [remote(line, x, line.at[x], 9 + d, (row_of(0, d), z)) for d in (1, 2, 3)]
         for one in lines:
             one.start()
+        for dz in (1, 2, 3):
+            source = lax.rem(z - dz + SIDE, SIDE)
+            remote(parts, source, part.at[0], 6 + dz, column_device(dz, 0)).wait_recv()
+        density_ref[...] = parts[0] + parts[1] + parts[2] + parts[3]
         for d in (1, 2, 3):
             source = lax.rem(x - d + SIDE, SIDE)
             remote(line, source, line.at[source], 9 + d, (row_of(0, d), z)).wait_recv()

time: 95.7 us -> 93.9 us (0.981)
  Pallas kernels: 90.3 us -> 88.4 us
    pallas_call x1, Pallas kernels: 90.3 us -> 88.4 us  [shards(): pl.pallas_call(kernel, grid=(batches // UNROLL,), in_specs=[pl.BlockSpec(...]
where the time goes in v6:
time: 93.9 us; the launch traced here: 93.6 us
  Pallas kernels  88.4 us (94%)
  local copies, waits for them, and re-layouts  2.92 us (3%)
  other arithmetic  1.66 us (2%)
    pallas_call x1, Pallas kernels, shards(): pl.pallas_call(kernel, grid=(batches // UNROLL,), in_specs=[pl.BlockSpec(...  88.4 us
    unnamed x7, local copies, waits for them, and re-layouts  2.92 us

profile of v6, /device:TPU:0, one launch (start us, length us, event | category | flops | bytes accessed | tf_op | source)
XLA Modules:
  0.0 93.6 jit_solution(4942920402248119991)
XLA Ops:
  0.6 1.0 %fusion.5 = s32[5,4,8,128]{3,2,1,0:T(8,128)S(1)} fusion(s32[40,512]{1,0:T(8,128)} %param.10, s32[]{:T(128)S(6)} %mul.17, s32[40]{0:T(128)} %param.11), kind=kLoop, calls=%fused_computation.7 | loop fusion | flops 368640 | bytes 164004
  1.7 0.7 fusion.7.member_ref
  2.3 0.0 copy-start
  2.3 1.0 %copy-done = bf16[192,1024]{1,0:T(8,128)(2,1)S(1)} copy-done((bf16[192,1024]{1,0:T(8,128)(2,1)S(1)}, bf16[192,1024]{1,0:T(8,128)(2,1)}, u32[]{:S(2)}) %copy-start) | copy-done | bytes 393240
  3.3 0.0 copy-start.1
  3.3 0.7 copy-done.1
  4.0 88.4 %shard_map.86 = (f32[40,128]{1,0:T(8,128)S(1)}, f32[49,64]{1,0:T(8,128)S(1)}) custom-call(s32[20480]{0:T(1024)S(1)} %bitcast.6, bf16[192,1024]{1,0:T(8,128)(2,1)S(1)} %copy-done, f32[8,128]{1,0:T(8,128)S(1)} %bitcast.8, bf16[40,512,512]{2,1,0:T(8,128)(2,1)} %m_hbm.1, f32[49,40,512]{2,1,0:T(8,128)} %bitcast.9, f32[64,40]{1,0:T(8,128)S(1)} %fusion.7.member_ref), custom_call_target="tpu_custom_call" | custom-call | tf_op jit(solution)/shard_map/pallas_call | solution.py:286
  92.4 0.6 copy.12
  93.0 0.6 copy.13
  (1 shorter events, 0.0 us)
Async XLA Ops:
  2.3 1.0 %copy-start = (bf16[192,1024]{1,0:T(8,128)(2,1)S(1)}, bf16[192,1024]{1,0:T(8,128)(2,1)}, u32[]{:S(2)}) copy-start(bf16[192,1024]{1,0:T(8,128)(2,1)} %coeffs_ref.1) | copy-start | bytes 1179652
  3.3 0.7 copy-start.1
